TPU v7x, 32 devices: a whole 2x2x4 slice. The times are simulated.
32 devices in a mesh: dp: 8 (over z, y), tensor: 4 (over x, core).
Axes of the slice: x: 2, y: 2, z: 4, core: 2. Of those that a mesh axis runs over, the one named last changes fastest.
Arguments:
- hidden_in: bfloat16 [16384, 768], P(('dp', 'tensor')), may hold values from -6 to 6
- lengths: int32 [16], P('dp'), may hold values from 1 to 1024, as said below
- ln1_gain: float32 [768], replicated, may hold values from 0.5 to 1.5
- ln1_shift: float32 [768], replicated, may hold values from -1.75 to 1.75
- qkv_weight: bfloat16 [3, 768, 768], P(None, None, 'tensor'), may hold values from -0.21875 to 0.21875
- qv_bias: float32 [2, 768], P(None, 'tensor'), may hold values from -3 to 3
- out_weight: bfloat16 [768, 768], P('tensor'), may hold values from -1.75 to 1.75
- out_bias: float32 [768], replicated, may hold values from -1.75 to 1.75
- ln2_gain: float32 [768], replicated, may hold values from 0.5 to 1.5
- ln2_shift: float32 [768], replicated, may hold values from -1.75 to 1.75
- up_weight: bfloat16 [768, 3072], P(None, 'tensor'), may hold values from -0.21875 to 0.21875
- up_bias: bfloat16 [3072], P('tensor'), may hold values from -3 to 3
- down_weight: bfloat16 [3072, 768], P('tensor'), may hold values from -0.109375 to 0.109375
- down_bias: float32 [768], replicated, may hold values from -1.75 to 1.75
- out_grad: bfloat16 [16384, 768], P(('dp', 'tensor')), may hold values from -6 to 6
Outputs:
- output: bfloat16 [16384, 768], P(('dp', 'tensor'))
- input_grad: bfloat16 [16384, 768], P(('dp', 'tensor'))
- ln1_gain_grad: float32 [768], replicated
- ln1_shift_grad: float32 [768], replicated
- qkv_weight_grad: float32 [3, 768, 768], P(None, None, 'tensor')
- qv_bias_grad: float32 [2, 768], P(None, 'tensor')
- out_weight_grad: float32 [768, 768], P('tensor')
- out_bias_grad: float32 [768], replicated
- ln2_gain_grad: float32 [768], replicated
- ln2_shift_grad: float32 [768], replicated
- up_weight_grad: float32 [768, 3072], P(None, 'tensor')
- up_bias_grad: float32 [3072], P('tensor')
- down_weight_grad: float32 [3072, 768], P('tensor')
- down_bias_grad: float32 [768], replicated
Inputs may be any that keep to these rules, and one draw needn't show every extreme that they name: `lengths`: some slot's length is exactly 1024.
All inputs are finite; a program needn't handle non-finite values.
Results may differ from a plain program's by a relative error of at most 0.012.
The roundings to bfloat16 on the way count: a program that leaves them out, or rounds other values in their place, can miss the bound.
Values may be sent and summed in bfloat16 or wider, within the bound.
A program may use at most 192 MiB of HBM per device.

v0:
```python
import math

import jax
import jax.numpy as jnp
from jax import lax
from jax.experimental import pallas as pl
from jax.experimental.pallas import tpu as pltpu
from jax.sharding import PartitionSpec as P

HD = 64
BLK = 256
BIG = 1e30
sel_factor = 4.0
score_scale = 1.0 / math.sqrt(HD)
f32 = jnp.float32
bf16 = jnp.bfloat16


def mm(a, b):
    return lax.dot_general(a, b, (((1,), (0,)), ((), ())), preferred_element_type=f32)


def mm_nt(a, b):
    return lax.dot_general(a, b, (((1,), (1,)), ((), ())), preferred_element_type=f32)


def flip(a):
    return a.astype(f32).T.astype(bf16)


def split_mm(tri, x):
    hi = x.astype(bf16)
    lo = (x - hi.astype(f32)).astype(bf16)
    return mm(tri, hi) + mm(tri, lo)


def head_mask(h, width):
    return lax.broadcasted_iota(jnp.int32, (BLK, width), 1) // HD == h


def masked_rows(x, mask, scale):
    return jnp.where(mask, x.astype(f32) * scale, 0.0).astype(bf16)


def fwd_block(i, heads, first, q_ref, k_ref, v_ref, fence, o_ref, lse_ref):
    width = q_ref.shape[1]
    cols = (i + 1) * BLK
    keys = k_ref[:cols, :]
    vals = v_ref[:cols, :]
    fenced = fence[:, :cols]
    lane = lax.broadcasted_iota(jnp.int32, (BLK, 128), 1)
    lse_ref[...] = jnp.zeros_like(lse_ref)
    out_scr = first

    def head(h, _):
        mask = head_mask(h, width)
        s = mm_nt(masked_rows(q_ref[...], mask, score_scale), keys) - fenced
        top = jnp.max(s, -1, keepdims=True)
        e = jnp.exp(s - top)
        total = jnp.sum(e, -1, keepdims=True)
        p = (e * (1.0 / total)).astype(bf16)
        out = mm(p, vals)
        out_scr[...] = jnp.where(mask, out, out_scr[...])
        lse_ref[...] = jnp.where(lane == h, top + jnp.log(total), lse_ref[...])
        return 0

    lax.fori_loop(0, heads, head, 0)
    o_ref[...] = out_scr[...].astype(bf16)


def make_fence(i, seq_len, length, sq_ref, sk_ref, fence, carry):
    cols = (i + 1) * BLK
    s0 = mm_nt(sq_ref[...], sk_ref[:cols, :]) * score_scale
    row = i * BLK + lax.broadcasted_iota(jnp.int32, (BLK, cols), 0)
    col = lax.broadcasted_iota(jnp.int32, (BLK, cols), 1)
    picked = (col >= 1) & (col < row)
    sel = jnp.where(picked, jnp.maximum(s0, 0.0), 0.0) * (sel_factor / seq_len)
    r2 = lax.broadcasted_iota(jnp.int32, (BLK, BLK), 0)
    c2 = lax.broadcasted_iota(jnp.int32, (BLK, BLK), 1)
    tri = jnp.where(c2 < r2, 1.0, 0.0).astype(bf16)
    total = carry[0:1, :cols] + split_mm(tri, sel)
    carry[0:1, :cols] = total[BLK - 1 : BLK, :] + sel[BLK - 1 : BLK, :]
    fence[:, :cols] = jnp.where((col <= row) & (col < length), total, BIG)


def fwd_first_kernel(heads, len_ref, q_ref, k_ref, v_ref, sq_ref, sk_ref, o_ref, lse_ref, f_ref, out_scr, carry):
    r = pl.program_id(0)
    seq_len = k_ref.shape[0]

    @pl.when(r == 0)
    def _():
        carry[...] = jnp.zeros_like(carry)

    for i in range(seq_len // BLK):

        @pl.when(r == i)
        def _():
            make_fence(i, seq_len, len_ref[0], sq_ref, sk_ref, f_ref, carry)
            fwd_block(i, heads, out_scr, q_ref, k_ref, v_ref, f_ref, o_ref, lse_ref)


def fwd_next_kernel(heads, q_ref, k_ref, v_ref, f_ref, o_ref, lse_ref, out_scr):
    r = pl.program_id(0)
    for i in range(k_ref.shape[0] // BLK):

        @pl.when(r == i)
        def _():
            fwd_block(i, heads, out_scr, q_ref, k_ref, v_ref, f_ref, o_ref, lse_ref)


def row_spec(width, back=None):
    if back is None:
        return pl.BlockSpec((BLK, width), lambda r: (r, 0))
    return pl.BlockSpec((BLK, width), lambda r: (back - 1 - r, 0))


def full_spec(rows, width):
    return pl.BlockSpec((rows, width), lambda r: (0, 0))


def attend_first(q, k, v, sq, sk, length):
    n, width = q.shape
    heads = width // HD
    return pl.pallas_call(
        lambda *refs: fwd_first_kernel(heads, *refs),
        grid=(n // BLK,),
        in_specs=[
            pl.BlockSpec(memory_space=pltpu.SMEM),
            row_spec(width),
            full_spec(n, width),
            full_spec(n, width),
            row_spec(HD),
            full_spec(n, HD),
        ],
        out_specs=[row_spec(width), row_spec(128), row_spec(n)],
        out_shape=[
            jax.ShapeDtypeStruct((n, width), bf16),
            jax.ShapeDtypeStruct((n, 128), f32),
            jax.ShapeDtypeStruct((n, n), f32),
        ],
        scratch_shapes=[pltpu.VMEM((BLK, width), f32), pltpu.VMEM((8, n), f32)],
        name="attend_first",
        cost_estimate=pl.CostEstimate(flops=6 * n * n * 256, bytes_accessed=8 * n * n, transcendentals=0),
    )(length, q, k, v, sq, sk)


def attend_next(q, k, v, fence):
    n, width = q.shape
    heads = width // HD
    return pl.pallas_call(
        lambda *refs: fwd_next_kernel(heads, *refs),
        grid=(n // BLK,),
        in_specs=[row_spec(width), full_spec(n, width), full_spec(n, width), row_spec(n)],
        out_specs=[row_spec(width), row_spec(128)],
        out_shape=[
            jax.ShapeDtypeStruct((n, width), bf16),
            jax.ShapeDtypeStruct((n, 128), f32),
        ],
        scratch_shapes=[pltpu.VMEM((BLK, width), f32)],
        name="attend_next",
        cost_estimate=pl.CostEstimate(flops=6 * n * n * 256, bytes_accessed=8 * n * n, transcendentals=0),
    )(q, k, v, fence)


def bwd_block(i, heads, q_ref, k_ref, v_ref, do_ref, lse_ref, f_ref, sq_ref, sk_ref,
              dq_ref, dsq_ref, dq_scr, dkt, dvt, dskt, later, fsum, qt, dot_):
    width = q_ref.shape[1]
    seq_len = k_ref.shape[0]
    cols = (i + 1) * BLK
    keys = k_ref[:cols, :]
    vals = v_ref[:cols, :]
    lane = lax.broadcasted_iota(jnp.int32, (BLK, 128), 1)
    qt[...] = (q_ref[...].astype(f32) * score_scale).T.astype(bf16)
    dot_[...] = flip(do_ref[...])
    fsum[:, :cols] = jnp.zeros((BLK, cols), f32)

    def head(h, _):
        mask = head_mask(h, width)
        lse = jnp.sum(jnp.where(lane == h, lse_ref[...], 0.0), -1, keepdims=True)
        s = mm_nt(masked_rows(q_ref[...], mask, score_scale), keys)
        p = jnp.exp(s - f_ref[:, :cols] - lse)
        dp = mm_nt(masked_rows(do_ref[...], mask, 1.0), vals)
        delta = jnp.sum(p * dp, -1, keepdims=True)
        g = (p * (dp - delta)).astype(bf16)
        rows = pl.ds(pl.multiple_of(h * HD, HD), HD)
        dq_scr[...] = jnp.where(mask, mm(g, keys), dq_scr[...])
        dkt[rows, :cols] += mm(qt[rows, :], g)
        dvt[rows, :cols] += mm(dot_[rows, :], p.astype(bf16))
        fsum[:, :cols] += g.astype(f32)
        return 0

    lax.fori_loop(0, heads, head, 0)
    dq_ref[...] = (dq_scr[...] * score_scale).astype(bf16)
    grad = -fsum[:, :cols]
    r2 = lax.broadcasted_iota(jnp.int32, (BLK, BLK), 0)
    c2 = lax.broadcasted_iota(jnp.int32, (BLK, BLK), 1)
    tri = jnp.where(c2 > r2, 1.0, 0.0).astype(bf16)
    dsel = later[0:1, :cols] + split_mm(tri, grad)
    later[0:1, :cols] = dsel[0:1, :] + grad[0:1, :]
    s0 = mm_nt(sq_ref[...], sk_ref[:cols, :])
    row = i * BLK + lax.broadcasted_iota(jnp.int32, (BLK, cols), 0)
    col = lax.broadcasted_iota(jnp.int32, (BLK, cols), 1)
    keep = (col >= 1) & (col < row) & (s0 > 0)
    gsel = jnp.where(keep, dsel * (sel_factor / seq_len), 0.0).astype(bf16)
    dsq_ref[...] = mm(gsel, sk_ref[:cols, :]) * score_scale
    sqt = (sq_ref[...].astype(f32) * score_scale).T.astype(bf16)
    dskt[:, :cols] += mm(sqt, gsel)


def bwd_kernel(heads, q_ref, k_ref, v_ref, do_ref, lse_ref, f_ref, sq_ref, sk_ref,
               dq_ref, dk_ref, dv_ref, dsq_ref, dsk_ref,
               dq_scr, dkt, dvt, dskt, later, fsum, qt, dot_):
    g = pl.program_id(0)
    n = k_ref.shape[0] // BLK

    @pl.when(g == 0)
    def _():
        dkt[...] = jnp.zeros_like(dkt)
        dvt[...] = jnp.zeros_like(dvt)
        dskt[...] = jnp.zeros_like(dskt)
        later[...] = jnp.zeros_like(later)

    for i in range(n):

        @pl.when(g == n - 1 - i)
        def _():
            bwd_block(i, heads, q_ref, k_ref, v_ref, do_ref, lse_ref, f_ref, sq_ref, sk_ref,
                      dq_ref, dsq_ref, dq_scr, dkt, dvt, dskt, later, fsum, qt, dot_)

    @pl.when(g == n - 1)
    def _():
        dk_ref[...] = dkt[...].T.astype(bf16)
        dv_ref[...] = dvt[...].T.astype(bf16)
        dsk_ref[...] = dskt[...].T


def attend_back(q, k, v, do, lse, fence, sq, sk):
    n, width = q.shape
    heads = width // HD
    back = n // BLK
    return pl.pallas_call(
        lambda *refs: bwd_kernel(heads, *refs),
        grid=(back,),
        in_specs=[
            row_spec(width, back),
            full_spec(n, width),
            full_spec(n, width),
            row_spec(width, back),
            row_spec(128, back),
            row_spec(n, back),
            row_spec(HD, back),
            full_spec(n, HD),
        ],
        out_specs=[
            row_spec(width, back),
            full_spec(n, width),
            full_spec(n, width),
            row_spec(HD, back),
            full_spec(n, HD),
        ],
        out_shape=[
            jax.ShapeDtypeStruct((n, width), bf16),
            jax.ShapeDtypeStruct((n, width), bf16),
            jax.ShapeDtypeStruct((n, width), bf16),
            jax.ShapeDtypeStruct((n, HD), f32),
            jax.ShapeDtypeStruct((n, HD), f32),
        ],
        scratch_shapes=[
            pltpu.VMEM((BLK, width), f32),
            pltpu.VMEM((width, n), f32),
            pltpu.VMEM((width, n), f32),
            pltpu.VMEM((HD, n), f32),
            pltpu.VMEM((8, n), f32),
            pltpu.VMEM((BLK, n), f32),
            pltpu.VMEM((width, BLK), bf16),
            pltpu.VMEM((width, BLK), bf16),
        ],
        name="attend_back",
        cost_estimate=pl.CostEstimate(flops=18 * n * n * 256, bytes_accessed=8 * n * n, transcendentals=0),
    )(q, k, v, do, lse, fence, sq, sk)


epsilon = 1e-05


def layer_norm(source, scales, offset):
    centre = source - jnp.mean(source, -1, keepdims=True)
    spread = jnp.mean(centre * centre, -1, keepdims=True)
    return centre * lax.rsqrt(spread + epsilon) * scales + offset


def gelu_tanh(source):
    return jax.nn.gelu(source, approximate=True)


def mm_tn(a, b):
    return lax.dot_general(a, b, (((0,), (0,)), ((), ())), preferred_element_type=f32)


def swap_core(x):
    n = lax.axis_size("tensor")
    return lax.ppermute(x, "tensor", [(i, i ^ 1) for i in range(n)])


def swap_chip(x):
    n = lax.axis_size("tensor")
    return lax.ppermute(x, "tensor", [(i, i ^ 2) for i in range(n)])

def send(src, dst, send_sem, recv_sem, **where):
    copy = pltpu.make_async_remote_copy(
        src_ref=src,
        dst_ref=dst,
        send_sem=send_sem,
        recv_sem=recv_sem,
        device_id=where,
        device_id_type=pl.DeviceIdType.MESH,
    )
    copy.start()
    return copy


def meet(devices):
    barrier = pltpu.get_barrier_semaphore()
    for where in devices:
        pl.semaphore_signal(barrier, inc=1, device_id=where, device_id_type=pl.DeviceIdType.MESH)
    pl.semaphore_wait(barrier, len(devices))


def finish_kernel(
    n, chunk, piece,
    gb, ga, small_in, dq1, dk1, dv1, dq2, dk2, dv2, dsel, w1, w2, sel_w, hidden, gain, gmid,
    fb, fa, small_out, input_grad,
    ng_send, ng_recv, yb, ya, sb, sa, zb, za, own_b, tb,
    small, ys, ss, zs, ts, out_s,
    core_s, core_r, y_s, y_r, z_s, z_r, t_s, t_r, az_s, az_r, ay_s, ay_r,
):
    idx = lax.axis_index("dp")
    me = lax.axis_index("tensor")
    odd = lax.rem(me, 2)
    par = lax.rem(idx, 2)
    z = lax.div(idx, 2)
    m = n // 2
    half = m * chunk
    shalf = m * piece
    rows = hidden.shape[0]
    ranks = 4
    core = me + 1 - 2 * odd
    ydev = idx + 1 - 2 * par
    peers = [lax.rem(me + d, ranks) for d in range(1, ranks)]
    zdev = [lax.rem(z + d, m) for d in range(1, m)]
    meet(
        [{"tensor": p} for p in peers]
        + [{"dp": ydev}]
        + [{"dp": 2 * p + par} for p in zdev]
    )
    give = pl.multiple_of((1 - par) * half, half)
    keep = pl.multiple_of(par * half, half)
    cyb = send(gb.at[pl.ds(give, half)], yb, y_s.at[0], y_r.at[0], dp=ydev)
    cya = send(ga.at[pl.ds(give, half)], ya, y_s.at[1], y_r.at[1], dp=ydev)

    def normed_grad(start):
        part = pl.ds(pl.multiple_of(start, rows), rows)
        total = mm_nt(dsel[part, :], sel_w[...])
        for grads, weights in (((dq1, dk1, dv1), w1), ((dq2, dk2, dv2), w2)):
            for j in range(3):
                total = total + mm_nt(grads[j][part, :], weights[j])
        return total

    ng_send[...] = normed_grad((1 - odd) * rows).astype(bf16)
    ccore = send(ng_send, ng_recv, core_s, core_r, tensor=core)
    grad = normed_grad(odd * rows)
    x = hidden[...].astype(f32)
    centre = x - jnp.mean(x, -1, keepdims=True)
    r = lax.rsqrt(jnp.mean(centre * centre, -1, keepdims=True) + epsilon)
    xhat = centre * r
    ccore.wait_recv()
    grad = grad + ng_recv[...].astype(f32)
    e = grad * gain[...]
    back = r * (e - jnp.mean(e, -1, keepdims=True) - xhat * jnp.mean(e * xhat, -1, keepdims=True))
    input_grad[...] = (gmid[...] + back).astype(bf16)
    small[...] = small_in[...]
    dgain = jnp.sum(grad * xhat, 0, keepdims=True)
    dshift = jnp.sum(grad, 0, keepdims=True)
    lines = dgain.shape[1] // 128
    for j in range(lines):
        small[j : j + 1, :] = dgain[:, j * 128 : (j + 1) * 128]
        small[lines + j : lines + j + 1, :] = dshift[:, j * 128 : (j + 1) * 128]
    sgive = pl.multiple_of((1 - par) * shalf, shalf)
    skeep = pl.multiple_of(par * shalf, shalf)
    cys = send(small.at[pl.ds(sgive, shalf)], ys, y_s.at[2], y_r.at[2], dp=ydev)

    def z_stage(total, recv, size, k):
        return [
            send(
                total.at[pl.ds(pl.multiple_of(zdev[d] * size, size), size)],
                recv.at[d],
                z_s.at[k, d],
                z_r.at[k, d],
                dp=2 * zdev[d] + par,
            )
            for d in range(m - 1)
        ]

    cyb.wait_recv()
    sb[...] = (gb[pl.ds(keep, half), :].astype(f32) + yb[...].astype(f32)).astype(bf16)
    czb = z_stage(sb, zb, chunk, 0)
    cys.wait_recv()
    ss[...] = small[pl.ds(skeep, shalf), :] + ys[...]
    czs = z_stage(ss, zs, piece, 2)
    cya.wait_recv()
    sa[...] = (ga[pl.ds(keep, half), :].astype(f32) + ya[...].astype(f32)).astype(bf16)
    cza = z_stage(sa, za, chunk, 1)

    def z_sum(total, recv, size, copies):
        acc = total[pl.ds(pl.multiple_of(z * size, size), size), :].astype(f32)
        for d in range(m - 1):
            copies[d].wait_recv()
            acc = acc + recv[d].astype(f32)
        return acc

    acc_b = z_sum(sb, zb, chunk, czb)
    own_b[...] = acc_b[:, :384]
    tb[me] = acc_b[:, 384:].astype(bf16)
    ts[me] = z_sum(ss, zs, piece, czs)
    ct = []
    for d in range(ranks - 1):
        ct.append(send(tb.at[me], tb.at[me], t_s.at[0, d], t_r.at[0, d], tensor=peers[d]))
        ct.append(send(ts.at[me], ts.at[me], t_s.at[1, d], t_r.at[1, d], tensor=peers[d]))
    at = par * m + z
    mine = pl.ds(pl.multiple_of(at * chunk, chunk), chunk)
    smine = pl.ds(pl.multiple_of(at * piece, piece), piece)

    def spread(full, where, k):
        out = [
            send(full.at[where], full.at[where], az_s.at[k, d], az_r.at[k, d], dp=2 * zdev[d] + par)
            for d in range(m - 1)
        ]
        return out, [send(full.at[where], full.at[where], ay_s.at[k, 0], ay_r.at[k, 0], dp=ydev)]

    def forward(full, size, k, copies, ahead):
        for d in range(m - 1):
            copies[d].wait_recv()
            came = par * m + lax.rem(z - (d + 1) + m, m)
            where = pl.ds(pl.multiple_of(came * size, size), size)
            ahead.append(
                send(full.at[where], full.at[where], ay_s.at[k, d + 1], ay_r.at[k, d + 1], dp=ydev)
            )

    fa[mine, :] = z_sum(sa, za, chunk, cza).astype(bf16)
    aza, aya = spread(fa, mine, 1)
    for c in ct:
        c.wait_recv()
    sel = tb[0].astype(f32)
    vec = ts[0]
    for d in range(1, ranks):
        sel = sel + tb[d].astype(f32)
        vec = vec + ts[d]
    first = jnp.where(me == 0, 1.0, 0.0)
    lane = lax.broadcasted_iota(jnp.int32, sel.shape, 1)
    lower = jnp.where(lane < HD, sel, 0.0) * first
    upper = jnp.where(lane < HD, 0.0, sel) * first
    fb[mine, :128] = (own_b[:, :128] + lower).astype(bf16)
    fb[mine, 128:256] = (own_b[:, 128:256] + upper).astype(bf16)
    fb[mine, 256:] = own_b[:, 256:].astype(bf16)
    azb, ayb = spread(fb, mine, 0)
    out_s[smine, :] = vec
    azs, ays = spread(out_s, smine, 2)
    forward(fa, chunk, 1, aza, aya)
    forward(fb, chunk, 0, azb, ayb)
    forward(out_s, piece, 2, azs, ays)
    for c in aya + ayb + ays:
        c.wait_recv()
    small_out[...] = out_s[...]
    for c in [cyb, cya, cys, ccore] + czb + cza + czs + ct + aza + azb + azs + aya + ayb + ays:
        c.wait_send()


def finish(n, gb, ga, small, grads1, grads2, dsel, w1, w2, sel_w, hidden, gain, gmid):
    m = n // 2
    chunk = gb.shape[0] // n
    piece = small.shape[0] // n
    rows, depth = hidden.shape
    half, shalf = m * chunk, m * piece
    wb, wa = gb.shape[1], ga.shape[1]
    ranks = 4
    vmem = pl.BlockSpec(memory_space=pltpu.VMEM)
    dma = pltpu.SemaphoreType.DMA
    return pl.pallas_call(
        lambda *refs: finish_kernel(n, chunk, piece, *refs),
        in_specs=[vmem] * 16,
        out_specs=[vmem] * 4,
        out_shape=[
            jax.ShapeDtypeStruct((n * chunk, wb - 128), bf16),
            jax.ShapeDtypeStruct((n * chunk, wa), bf16),
            jax.ShapeDtypeStruct(small.shape, f32),
            jax.ShapeDtypeStruct((rows, depth), bf16),
        ],
        scratch_shapes=[
            pltpu.VMEM((rows, depth), bf16),
            pltpu.VMEM((rows, depth), bf16),
            pltpu.VMEM((half, wb), bf16),
            pltpu.VMEM((half, wa), bf16),
            pltpu.VMEM((half, wb), bf16),
            pltpu.VMEM((half, wa), bf16),
            pltpu.VMEM((m - 1, chunk, wb), bf16),
            pltpu.VMEM((m - 1, chunk, wa), bf16),
            pltpu.VMEM((chunk, wb - 128), f32),
            pltpu.VMEM((ranks, chunk, 128), bf16),
            pltpu.VMEM(small.shape, f32),
            pltpu.VMEM((shalf, 128), f32),
            pltpu.VMEM((shalf, 128), f32),
            pltpu.VMEM((m - 1, piece, 128), f32),
            pltpu.VMEM((ranks, piece, 128), f32),
            pltpu.VMEM(small.shape, f32),
            dma, dma,
            dma((3,)), dma((3,)),
            dma((3, m - 1)), dma((3, m - 1)),
            dma((2, 3)), dma((2, 3)),
            dma((3, m - 1)), dma((3, m - 1)),
            dma((3, m)), dma((3, m)),
        ],
        compiler_params=pltpu.CompilerParams(
            collective_id=0, has_side_effects=True, vmem_limit_bytes=60 * 1024 * 1024
        ),
        name="finish",
    )(gb, ga, small, *grads1, *grads2, dsel, w1, w2, sel_w, hidden, gain, gmid)


def shards(
    hidden_in,
    lengths,
    ln1_gain,
    ln1_shift,
    qkv_weight,
    qv_bias,
    out_weight,
    out_bias,
    ln2_gain,
    ln2_shift,
    up_weight,
    up_bias,
    down_weight,
    down_bias,
    out_grad,
):
    rows = hidden_in.shape[0]
    ranks = lax.axis_size("tensor")
    me = lax.axis_index("tensor")
    odd = me % 2
    length = jnp.where(me < 2, lengths[0], lengths[1])
    live = (odd * rows + jnp.arange(rows) < length).astype(f32)[:, None]

    def join(mine, other):
        first = jnp.where(odd == 0, mine, other)
        second = jnp.where(odd == 0, other, mine)
        return jnp.concatenate([first, second], 0)

    def my_half(x):
        return lax.dynamic_slice_in_dim(x, odd * rows, rows, 0)

    def other_half(x):
        return lax.dynamic_slice_in_dim(x, (1 - odd) * rows, rows, 0)

    sel_w = jnp.concatenate([qkv_weight[0][:, :HD], qkv_weight[1][:, :HD]], 1)
    sel_b = qv_bias[:1, :HD]
    sel_w = jnp.where(me == 0, sel_w, lax.ppermute(sel_w, "tensor", [(0, 2)]))
    sel_b = jnp.where(me == 0, sel_b, lax.ppermute(sel_b, "tensor", [(0, 2)]))
    sel_w = jnp.where(odd == 0, sel_w, lax.ppermute(sel_w, "tensor", [(0, 1), (2, 3)]))
    sel_b = jnp.where(odd == 0, sel_b, lax.ppermute(sel_b, "tensor", [(0, 1), (2, 3)]))

    residual = hidden_in.astype(f32)
    normed_mine = layer_norm(residual, ln1_gain, ln1_shift).astype(bf16)
    normed = join(normed_mine, swap_core(normed_mine))

    qkv_far = swap_chip(qkv_weight)
    bias_far = swap_chip(qv_bias)
    out_far = swap_chip(out_weight)

    grad_out = out_grad.astype(f32) * live
    grad_branch = grad_out.astype(bf16)
    grad_near = join(grad_branch, swap_core(grad_branch))
    grad_far = swap_chip(grad_branch)
    grad_far = join(grad_far, swap_core(grad_far))

    def project(weights, bias):
        q = (mm(normed, weights[0]) + bias[0]).astype(bf16)
        k = mm(normed, weights[1]).astype(bf16)
        v = (mm(normed, weights[2]) + bias[1]).astype(bf16)
        return q, k, v

    sq = (mm(normed, sel_w[:, :HD]) + sel_b).astype(bf16)
    sk = mm(normed, sel_w[:, HD:]).astype(bf16)
    q1, k1, v1 = project(qkv_weight, qv_bias)
    o1, lse1, fence = attend_first(q1, k1, v1, sq, sk, length[None])
    q2, k2, v2 = project(qkv_far, bias_far)
    o2, lse2 = attend_next(q2, k2, v2, fence)

    def attn_out(part):
        return mm(part(o1), out_weight) + mm(part(o2), out_far)

    attn_given = swap_core(attn_out(other_half).astype(bf16))
    middle = residual + (attn_out(my_half) + attn_given.astype(f32)) + out_bias
    inner, ln2_back = jax.vjp(layer_norm, middle, ln2_gain, ln2_shift)
    inner = inner.astype(bf16)
    inner_near = join(inner, swap_core(inner))
    inner_far = swap_chip(inner)
    inner_far = join(inner_far, swap_core(inner_far))

    def feed(inner_rows, grad_rows):
        pre = mm(inner_rows, up_weight) + up_bias.astype(f32)
        act, gelu_back = jax.vjp(gelu_tanh, pre)
        grad_act = mm_nt(grad_rows, down_weight)
        grad_pre = gelu_back(grad_act)[0].astype(bf16)
        return act.astype(bf16), grad_pre

    act_near, pre_near = feed(inner_near, grad_near)
    act_far, pre_far = feed(inner_far, grad_far)

    def gather_sum(near, far, weight, product):
        far_given = swap_core(product(other_half(far), weight).astype(bf16))
        far_sum = product(my_half(far), weight) + far_given.astype(f32)
        from_chip = swap_chip(far_sum.astype(bf16))
        near_given = swap_core(product(other_half(near), weight).astype(bf16))
        return product(my_half(near), weight) + near_given.astype(f32) + from_chip.astype(f32)

    grad_inner = gather_sum(pre_near, pre_far, up_weight, mm_nt)
    branch = gather_sum(act_near, act_far, down_weight, mm)
    output = (live * (middle + branch + down_bias)).astype(bf16)

    down_grad = mm_tn(act_near, grad_near) + mm_tn(act_far, grad_far)
    up_grad = mm_tn(inner_near, pre_near) + mm_tn(inner_far, pre_far)
    up_bias_grad = jnp.sum(pre_near, 0, dtype=f32) + jnp.sum(pre_far, 0, dtype=f32)

    grad_norm2, ln2_gain_grad, ln2_shift_grad = ln2_back(grad_inner)
    grad_middle = grad_out + grad_norm2
    grad_attn = grad_middle.astype(bf16)
    out_bias_grad = jnp.sum(grad_attn, 0, dtype=f32)
    down_bias_grad = jnp.sum(grad_out, 0)
    attn_rows = join(grad_attn, swap_core(grad_attn))

    go2 = mm_nt(attn_rows, out_far).astype(bf16)
    go1 = mm_nt(attn_rows, out_weight).astype(bf16)
    dq2, dk2, dv2, dsq2, dsk2 = attend_back(q2, k2, v2, go2, lse2, fence, sq, sk)
    dq1, dk1, dv1, dsq1, dsk1 = attend_back(q1, k1, v1, go1, lse1, fence, sq, sk)

    def grad_block(dq, dk, dv, o):
        return jnp.concatenate(
            [mm_tn(normed, dq), mm_tn(normed, dk), mm_tn(normed, dv), mm_tn(attn_rows, o)], 1
        )

    n = lax.axis_size("dp")
    width = q1.shape[1]
    depth = normed.shape[1]
    chunk = -(-depth // (16 * n)) * 16
    far_block = swap_chip(grad_block(dq2, dk2, dv2, o2).astype(bf16))
    block = grad_block(dq1, dk1, dv1, o1) + far_block.astype(f32)
    dsel = jnp.concatenate([dsq1 + dsq2, dsk1 + dsk2], 1).astype(bf16)
    sel_grad = mm_tn(normed, dsel)
    fill = ((0, n * chunk - depth), (0, 0))
    block_b = jnp.pad(jnp.concatenate([block[:, : 2 * width], sel_grad], 1), fill).astype(bf16)
    block_a = jnp.pad(block[:, 2 * width :], fill).astype(bf16)

    ffn_grad = lax.psum(jnp.concatenate([up_grad, down_grad], 0).astype(bf16), "dp").astype(f32)

    def bias_of(dq, dv):
        return jnp.stack([jnp.sum(dq, 0, dtype=f32), jnp.sum(dv, 0, dtype=f32)])

    slot = jnp.arange(ranks)[:, None, None]
    sel_bias = jnp.pad(jnp.sum(dsel[:, :HD], 0, dtype=f32)[None], ((0, 1), (0, width - HD)))
    qv_parts = (
        jnp.where(slot == me, bias_of(dq1, dv1)[None], 0.0)
        + jnp.where(slot == me ^ 2, bias_of(dq2, dv2)[None], 0.0)
        + jnp.where(slot == 0, sel_bias[None], 0.0)
    )
    up_parts = jnp.where(slot[:, 0] == me, up_bias_grad[None], 0.0)
    none = jnp.zeros_like(out_bias_grad)
    small = jnp.concatenate(
        [
            none,
            none,
            out_bias_grad,
            ln2_gain_grad,
            ln2_shift_grad,
            down_bias_grad,
            up_parts.reshape(-1),
            qv_parts.reshape(-1),
        ]
    )
    lines = small.shape[0] // 128
    piece = -(-lines // (8 * n)) * 8
    small = jnp.pad(small.reshape(lines, 128), ((0, n * piece - lines), (0, 0)))
    full_b, full_a, small, input_grad = finish(
        n, block_b, block_a, small, (dq1, dk1, dv1), (dq2, dk2, dv2), dsel,
        qkv_weight, qkv_far, sel_w, hidden_in, ln1_gain[None], grad_middle,
    )
    small = small[:lines].reshape(-1)
    vectors = small[: 6 * depth].reshape(6, depth)
    hidden = up_bias.shape[0]
    up_all = small[6 * depth : 6 * depth + ranks * hidden].reshape(ranks, hidden)
    qv_all = small[6 * depth + ranks * hidden :].reshape(ranks, 2, width)
    up_bias_grad = lax.dynamic_index_in_dim(up_all, me, 0, keepdims=False)
    qv_bias_grad = lax.dynamic_index_in_dim(qv_all, me, 0, keepdims=False)
    qkv_grad = jnp.stack(
        [full_b[:depth, :width], full_b[:depth, width:], full_a[:depth, :width]]
    ).astype(f32)
    out_weight_grad = full_a[:depth, width:].T.astype(f32)
    return (
        output,
        input_grad,
        vectors[0],
        vectors[1],
        qkv_grad,
        qv_bias_grad,
        out_weight_grad,
        vectors[2],
        vectors[3],
        vectors[4],
        ffn_grad[:depth],
        up_bias_grad,
        ffn_grad[depth:],
        vectors[5],
    )


def solution(mesh):
    return jax.shard_map(
        shards,
        mesh=mesh,
        in_specs=(
            P(("dp", "tensor"), None),
            P("dp"),
            P(),
            P(),
            P(None, None, "tensor"),
            P(None, "tensor"),
            P("tensor", None),
            P(),
            P(),
            P(),
            P(None, "tensor"),
            P("tensor"),
            P("tensor", None),
            P(),
            P(("dp", "tensor"), None),
        ),
        out_specs=(
            P(("dp", "tensor"), None),
            P(("dp", "tensor"), None),
            P(),
            P(),
            P(None, None, "tensor"),
            P(None, "tensor"),
            P("tensor", None),
            P(),
            P(),
            P(),
            P(None, "tensor"),
            P("tensor"),
            P("tensor", None),
            P(),
        ),
        check_vma=False,
    )
```

profile of v0, /device:TPU:0, one launch (start us, length us, event | category | flops | bytes accessed | tf_op | source)
XLA Modules:
  0.0 395.1 jit_solution(2173732958092624118)
XLA Ops:
  7.2 3.0 collective-permute-start.5
  10.3 1.5 copy.79.refs_10_
  12.8 2.8 collective-permute-start.1
  18.6 4.5 %collective-permute-start.3 = (f32[1,64]{1,0:T(1,128)}, f32[1,64]{1,0:T(1,128)}, u32[]{:S(2)}, u32[]{:S(2)}) collective-permute-start(f32[1,64]{1,0:T(1,128)} %slice.136), channel_id=1, source_target_pairs={{0,2},{4,6},{8,10},{12,14},{16,18},{20,22},{24,26},{28,30}} | collective-permute-start | bytes 776 | tf_op jit(solution)/shard_map/ppermute | solution.py:567
  26.3 5.3 %collective-permute-done.3 = f32[1,64]{1,0:T(1,128)} collective-permute-done((f32[1,64]{1,0:T(1,128)}, f32[1,64]{1,0:T(1,128)}, u32[]{:S(2)}, u32[]{:S(2)}) %collective-permute-start.3) | collective-permute-done | bytes 288 | tf_op jit(solution)/shard_map/ppermute | solution.py:567
  32.8 1.8 collective-permute-start.4
  35.0 2.5 collective-permute-start.7
  38.4 2.9 collective-permute-start.2
  42.6 1.7 broadcast_select_fusion.11
  45.8 2.4 fusion.25.refs_3_.refs_2_
  52.2 15.5 %attend_first.1 = (bf16[1024,192]{1,0:T(8,128)(2,1)}, f32[1024,128]{1,0:T(8,128)}, f32[1024,1024]{1,0:T(8,128)}) custom-call(s32[1]{0:T(128)} %bitcast.2.refs_0_, bf16[1024,192]{1,0:T(8,128)(2,1)} %fusion.24.refs_1_.refs_0_, bf16[1024,192]{1,0:T(8,128)(2,1)} %convolution_convert_fusion.5.refs_2_.refs_1_, bf16[1024,192]{1,0:T(8,128)(2,1)} %fusion.25.refs_3_.refs_2_, ...), custom_call_target="tpu_custom_call" | custom-call | flops 1610612736 | bytes 8388608 | tf_op jit(solution)/shard_map/attend_first/pallas_call | solution.py:124
  67.7 1.5 fusion.54
  69.3 2.4 fusion.26.refs_0_
  71.7 2.3 fusion.27.refs_2_
  74.0 2.4 convolution_convert_fusion.4.refs_1_
  76.4 12.6 %attend_next.1 = (bf16[1024,192]{1,0:T(8,128)(2,1)}, f32[1024,128]{1,0:T(8,128)}) custom-call(bf16[1024,192]{1,0:T(8,128)(2,1)} %fusion.26.refs_0_, bf16[1024,192]{1,0:T(8,128)(2,1)} %convolution_convert_fusion.4.refs_1_, bf16[1024,192]{1,0:T(8,128)(2,1)} %fusion.27.refs_2_, f32[1024,1024]{1,0:T(8,128)} %get-tuple-element.34.refs_3_.refs_5_), custom_call_target="tpu_custom_call" | custom-call | flops 1610612736 | bytes 8388608 | tf_op jit(solution)/shard_map/attend_next/pallas_call | solution.py:150
  89.0 2.4 add_convert_fusion.5
  94.5 1.6 fusion.92
  98.3 1.7 collective-permute-start.11
  100.0 13.2 %collective-permute-done.17 = bf16[512,768]{1,0:T(8,128)(2,1)} collective-permute-done((bf16[512,768]{1,0:T(8,128)(2,1)}, bf16[512,768]{1,0:T(8,128)(2,1)}, u32[]{:S(2)}, u32[]{:S(2)}) %collective-permute-start.17) | collective-permute-done | bytes 786464 | tf_op jit(solution)/shard_map/ppermute | solution.py:307
  118.6 10.9 %collective-permute-done.11 = bf16[512,768]{1,0:T(8,128)(2,1)} collective-permute-done((bf16[512,768]{1,0:T(8,128)(2,1)}, bf16[512,768]{1,0:T(8,128)(2,1)}, u32[]{:S(2)}, u32[]{:S(2)}) %collective-permute-start.11) | collective-permute-done | bytes 786464 | tf_op jit(solution)/shard_map/ppermute | solution.py:307
  129.6 2.7 broadcast_select_fusion.5
  132.2 2.5 copy.101.refs_11_
  136.3 1.6 broadcast_select_fusion.9
  140.9 2.8 multiply_convert_fusion.1
  143.8 4.6 %convert_reduce_fusion.1 = (f32[768]{0:T(1024)}, bf16[1024,768]{1,0:T(8,128)(2,1)S(1)}) fusion(f32[1024,768]{1,0:T(8,128)S(1)} %get-tuple-element.145, f32[768]{0:T(1024)S(1)} %copy-done.52, bf16[768,768]{1,0:T(8,128)(2,1)S(1)} %copy-done.60, bf16[512,768]{1,0:T(8,128)(2,1)S(1)} %copy-done.24, bf16[512,768]{1,0:T(8,128)(2,1)S(1)} %copy-done.23), kind=kOutput, calls=%fused_computation.19 | convolution fusion | flops 1229192448 | bytes 7477248 | tf_op jit(solution)/shard_map/dot_general | solution.py:24
  150.7 4.6 %convert_reduce_fusion = (f32[768]{0:T(1024)}, bf16[1024,768]{1,0:T(8,128)(2,1)S(1)}) fusion(f32[1024,768]{1,0:T(8,128)S(1)} %fusion.32, f32[768]{0:T(1024)S(1)} %copy-done.52, bf16[768,768]{1,0:T(8,128)(2,1)S(1)} %copy-done.60, bf16[512,768]{1,0:T(8,128)(2,1)S(1)} %get-tuple-element.115, bf16[512,768]{1,0:T(8,128)(2,1)S(1)} %get-tuple-element.114), kind=kOutput, calls=%fused_computation.18 | convolution fusion | flops 1229192448 | bytes 7477248 | tf_op jit(solution)/shard_map/dot_general | solution.py:24
  161.0 1.5 add_convert_fusion
  166.2 1.8 collective-permute-start.14
  168.8 15.9 %collective-permute-done.20 = bf16[512,768]{1,0:T(8,128)(2,1)S(1)} collective-permute-done((bf16[512,768]{1,0:T(8,128)(2,1)S(1)}, bf16[512,768]{1,0:T(8,128)(2,1)S(1)}, u32[]{:S(2)}, u32[]{:S(2)}) %collective-permute-start.20) | collective-permute-done | bytes 786464 | tf_op jit(solution)/shard_map/ppermute | solution.py:307
  185.5 15.5 %collective-permute-done.14 = bf16[512,768]{1,0:T(8,128)(2,1)S(1)} collective-permute-done((bf16[512,768]{1,0:T(8,128)(2,1)S(1)}, bf16[512,768]{1,0:T(8,128)(2,1)S(1)}, u32[]{:S(2)}, u32[]{:S(2)}) %collective-permute-start.14) | collective-permute-done | bytes 786464 | tf_op jit(solution)/shard_map/ppermute | solution.py:307
  201.0 1.7 fusion.91
  202.8 1.5 convert_reduce_fusion.3
  204.3 1.6 pad_maximum_fusion
  215.8 2.1 convolution_convert_fusion.6
  218.9 16.8 %attend_back.3 = (bf16[1024,192]{1,0:T(8,128)(2,1)}, bf16[1024,192]{1,0:T(8,128)(2,1)}, bf16[1024,192]{1,0:T(8,128)(2,1)}, f32[1024,64]{1,0:T(8,128)}, f32[1024,64]{1,0:T(8,128)}) custom-call(bf16[1024,192]{1,0:T(8,128)(2,1)} %fusion.26.refs_0_, bf16[1024,192]{1,0:T(8,128)(2,1)} %convolution_convert_fusion.4.refs_1_, bf16[1024,192]{1,0:T(8,128)(2,1)} %fusion.27.refs_2_, ...), custom_call_target="tpu_custom_call" | custom-call | flops 4831838208 | bytes 8388608 | tf_op jit(solution)/shard_map/attend_back/pallas_call | solution.py:241
  235.8 2.4 convolution_convert_fusion.11
  238.4 16.9 %attend_back.2 = (bf16[1024,192]{1,0:T(8,128)(2,1)}, bf16[1024,192]{1,0:T(8,128)(2,1)}, bf16[1024,192]{1,0:T(8,128)(2,1)}, f32[1024,64]{1,0:T(8,128)}, f32[1024,64]{1,0:T(8,128)}) custom-call(bf16[1024,192]{1,0:T(8,128)(2,1)} %fusion.24.refs_1_.refs_0_, bf16[1024,192]{1,0:T(8,128)(2,1)} %convolution_convert_fusion.5.refs_2_.refs_1_, ...), custom_call_target="tpu_custom_call" | custom-call | flops 4831838208 | bytes 8388608 | tf_op jit(solution)/shard_map/attend_back/pallas_call | solution.py:241
  262.6 2.0 convolution_convert_fusion.8
  271.3 1.5 fusion.88
  274.3 1.5 fusion.89
  275.8 39.4 %all-reduce.4.cloned.1.call-done = bf16[1536,768]{1,0:T(8,128)(2,1)} async-done(((bf16[1536,768]{1,0:T(8,128)(2,1)}), bf16[1536,768]{1,0:T(8,128)(2,1)}) %all-reduce.4.cloned.1.call-update) | async-done | bytes 2359312 | tf_op jit(solution)/shard_map/psum | solution.py:663
  315.1 4.3 %fusion.94 = (f32[768,768]{1,0:T(8,128)}, f32[768,768]{1,0:T(8,128)}) fusion(bf16[1536,768]{1,0:T(8,128)(2,1)} %all-reduce.4.cloned.1.call-done), kind=kLoop, calls=%fused_computation.208 | loop fusion | bytes 9437184 | tf_op jit(solution)/shard_map/slice | solution.py:720
  319.5 1.9 fusion.14
  323.2 51.6 %finish.1 = (bf16[768,384]{1,0:T(8,128)(2,1)}, bf16[768,384]{1,0:T(8,128)(2,1)}, f32[128,128]{1,0:T(8,128)}, bf16[512,768]{1,0:T(8,128)(2,1)}) custom-call(bf16[768,512]{1,0:T(8,128)(2,1)} %pad_maximum_fusion.20.refs_0_, bf16[768,384]{1,0:T(8,128)(2,1)} %get-tuple-element.122.refs_1_, f32[128,128]{1,0:T(8,128)} %pad.9.refs_2_, ...), custom_call_target="tpu_custom_call" | custom-call | tf_op jit(solution)/shard_map/finish/pallas_call | solution.py:488
  378.4 2.2 convert_bitcast_fusion
  381.1 1.8 copy.102
  382.9 2.3 copy.103
  (255 shorter events, 78.5 us)
Async XLA Ops:
  7.2 132.3 %copy-start = (bf16[768,768]{1,0:T(8,128)(2,1)S(1)}, bf16[768,768]{1,0:T(8,128)(2,1)}, u32[]{:S(2)}) copy-start(bf16[768,768]{1,0:T(8,128)(2,1)} %param.25) | copy-start | bytes 3538948
  7.2 307.9 %all-reduce.4.cloned.1.call-start = ((), (), s32[]{:S(2)}) async-start(), calls=%async_computation | async-start | bytes 4718592 | tf_op jit(solution)/shard_map/psum | solution.py:663
  7.2 62.0 %collective-permute-start.5 = (bf16[3,768,192]{1,2,0:T(8,128)(2,1)}, bf16[3,768,192]{1,2,0:T(8,128)(2,1)}, u32[]{:S(2)}, u32[]{:S(2)}) collective-permute-start(bf16[3,768,192]{1,2,0:T(8,128)(2,1)} %param.19), channel_id=1, source_target_pairs={{0,2},{1,3},{2,0},{3,1},{4,6},{5,7},{6,4},{7,5},{8,10},{9,11},{10,... | collective-permute-start | bytes 2654216 | tf_op jit(solution)/shard_map/ppermute | solution.py:307
  11.8 39.0 %copy-start.3 = (bf16[3,768,192]{2,1,0:T(8,128)(2,1)}, bf16[3,768,192]{2,1,0:T(8,128)(2,1)S(1)}, u32[]{:S(2)}) copy-start(bf16[3,768,192]{2,1,0:T(8,128)(2,1)S(1)} %copy.79.refs_10_) | copy-start | bytes 2654212
  11.8 3.7 copy-start.2
  11.9 4.2 %copy-start.41 = (f32[768]{0:T(1024)S(1)}, f32[768]{0:T(1024)}, u32[]{:S(2)}) copy-start(f32[768]{0:T(1024)} %param.17) | copy-start | bytes 9220
  11.9 4.2 %copy-start.44 = (f32[768]{0:T(1024)S(1)}, f32[768]{0:T(1024)}, u32[]{:S(2)}) copy-start(f32[768]{0:T(1024)} %param.18) | copy-start | bytes 9220
  12.8 11.6 %copy-start.53 = (s32[2]{0:T(128)S(1)}, s32[2]{0:T(128)}, u32[]{:S(2)}) copy-start(s32[2]{0:T(128)} %param.16) | copy-start | bytes 28
  12.8 25.4 %collective-permute-start.1 = (bf16[768,128]{1,0:T(8,128)(2,1)}, bf16[768,128]{1,0:T(8,128)(2,1)}, u32[]{:S(2)}, u32[]{:S(2)}) collective-permute-start(bf16[768,128]{1,0:T(8,128)(2,1)} %pad_maximum_fusion.22), channel_id=1, source_target_pairs={{0,2},{4,6},{8,10},{12,14},{16,18},{20,22},{24,26},{28,30}} | collective-permute-start | bytes 589832 | tf_op jit(solution)/shard_map/ppermute | solution.py:566
  17.4 25.2 %collective-permute-start = (bf16[512,768]{1,0:T(8,128)(2,1)}, bf16[512,768]{1,0:T(8,128)(2,1)}, u32[]{:S(2)}, u32[]{:S(2)}) collective-permute-start(bf16[512,768]{1,0:T(8,128)(2,1)} %fusion.20), channel_id=1, source_target_pairs={{0,1},{1,0},{2,3},{3,2},{4,5},{5,4},{6,7},{7,6},{8,9},{9,8},{10,11... | collective-permute-start | bytes 2359304 | tf_op jit(solution)/shard_map/ppermute | solution.py:302
  17.4 23.9 %collective-permute-start.6 = (f32[2,192]{1,0:T(2,128)}, f32[2,192]{1,0:T(2,128)}, u32[]{:S(2)}, u32[]{:S(2)}) collective-permute-start(f32[2,192]{1,0:T(2,128)} %param.20), channel_id=1, source_target_pairs={{0,2},{1,3},{2,0},{3,1},{4,6},{5,7},{6,4},{7,5},{8,10},{9,11},{10,... | collective-permute-start | bytes 4616 | tf_op jit(solution)/shard_map/ppermute | solution.py:307
  18.6 13.0 %collective-permute-start.3 = (f32[1,64]{1,0:T(1,128)}, f32[1,64]{1,0:T(1,128)}, u32[]{:S(2)}, u32[]{:S(2)}) collective-permute-start(f32[1,64]{1,0:T(1,128)} %slice.136), channel_id=1, source_target_pairs={{0,2},{4,6},{8,10},{12,14},{16,18},{20,22},{24,26},{28,30}} | collective-permute-start | bytes 776 | tf_op jit(solution)/shard_map/ppermute | solution.py:567
  32.8 2.2 collective-permute-start.4
  35.0 54.0 %collective-permute-start.7 = (bf16[192,768]{1,0:T(8,128)(2,1)}, bf16[192,768]{1,0:T(8,128)(2,1)}, u32[]{:S(2)}, u32[]{:S(2)}) collective-permute-start(bf16[192,768]{1,0:T(8,128)(2,1)} %param.21), channel_id=1, source_target_pairs={{0,2},{1,3},{2,0},{3,1},{4,6},{5,7},{6,4},{7,5},{8,10},{9,11},{10,... | collective-permute-start | bytes 884744 | tf_op jit(solution)/shard_map/ppermute | solution.py:307
  38.4 4.2 %collective-permute-start.2 = (bf16[768,128]{1,0:T(8,128)(2,1)S(1)}, bf16[768,128]{1,0:T(8,128)(2,1)S(1)}, u32[]{:S(2)}, u32[]{:S(2)}) collective-permute-start(bf16[768,128]{1,0:T(8,128)(2,1)S(1)} %broadcast_select_fusion.12), channel_id=1, source_target_pairs={{0,1},{2,3},{4,5},{6,7},{8,9},{10,11},{12,13},{14,15},{16,17},{18,... | collective-permute-start | bytes 589832 | tf_op jit(solution)/shard_map/ppermute | solution.py:568
  42.6 6.8 %copy-start.32 = (bf16[768,128]{1,0:T(8,128)(2,1)}, bf16[768,128]{1,0:T(8,128)(2,1)S(1)}, u32[]{:S(2)}) copy-start(bf16[768,128]{1,0:T(8,128)(2,1)S(1)} %broadcast_select_fusion.13.refs_12_) | copy-start | bytes 589828
  44.4 6.4 %copy-start.15 = (bf16[512,768]{1,0:T(8,128)(2,1)}, bf16[512,768]{1,0:T(8,128)(2,1)S(1)}, u32[]{:S(2)}) copy-start(bf16[512,768]{1,0:T(8,128)(2,1)S(1)} %get-tuple-element.120) | copy-start | bytes 2359300
  44.4 6.4 %copy-start.19 = (bf16[512,768]{1,0:T(8,128)(2,1)}, bf16[512,768]{1,0:T(8,128)(2,1)S(1)}, u32[]{:S(2)}) copy-start(bf16[512,768]{1,0:T(8,128)(2,1)S(1)} %get-tuple-element.121) | copy-start | bytes 2359300
  91.4 3.1 collective-permute-start.8
  92.5 20.7 %collective-permute-start.17 = (bf16[512,768]{1,0:T(8,128)(2,1)}, bf16[512,768]{1,0:T(8,128)(2,1)}, u32[]{:S(2)}, u32[]{:S(2)}) collective-permute-start(bf16[512,768]{1,0:T(8,128)(2,1)} %fusion.23), channel_id=1, source_target_pairs={{0,2},{1,3},{2,0},{3,1},{4,6},{5,7},{6,4},{7,5},{8,10},{9,11},{10,... | collective-permute-start | bytes 2359304 | tf_op jit(solution)/shard_map/ppermute | solution.py:307
  97.1 32.5 %copy-start.5 = (bf16[512,768]{1,0:T(8,128)(2,1)S(1)}, bf16[512,768]{1,0:T(8,128)(2,1)}, u32[]{:S(2)}) copy-start(bf16[512,768]{1,0:T(8,128)(2,1)} %param.29) | copy-start | bytes 2359300
  98.3 31.3 %collective-permute-start.11 = (bf16[512,768]{1,0:T(8,128)(2,1)}, bf16[512,768]{1,0:T(8,128)(2,1)}, u32[]{:S(2)}, u32[]{:S(2)}) collective-permute-start(bf16[512,768]{1,0:T(8,128)(2,1)} %add_convert_fusion.4), channel_id=1, source_target_pairs={{0,2},{1,3},{2,0},{3,1},{4,6},{5,7},{6,4},{7,5},{8,10},{9,11},{10,... | collective-permute-start | bytes 2359304 | tf_op jit(solution)/shard_map/ppermute | solution.py:307
  100.0 29.6 %collective-permute-start.15 = (bf16[512,768]{1,0:T(8,128)(2,1)}, bf16[512,768]{1,0:T(8,128)(2,1)}, u32[]{:S(2)}, u32[]{:S(2)}) collective-permute-start(bf16[512,768]{1,0:T(8,128)(2,1)} %fusion.23), channel_id=1, source_target_pairs={{0,1},{1,0},{2,3},{3,2},{4,5},{5,4},{6,7},{7,6},{8,9},{9,8},{10,11... | collective-permute-start | bytes 2359304 | tf_op jit(solution)/shard_map/ppermute | solution.py:302
  113.2 21.5 %collective-permute-start.18 = (bf16[512,768]{1,0:T(8,128)(2,1)}, bf16[512,768]{1,0:T(8,128)(2,1)}, u32[]{:S(2)}, u32[]{:S(2)}) collective-permute-start(bf16[512,768]{1,0:T(8,128)(2,1)} %collective-permute-done.17), channel_id=1, source_target_pairs={{0,1},{1,0},{2,3},{3,2},{4,5},{5,4},{6,7},{7,6},{8,9},{9,8},{10,11... | collective-permute-start | bytes 2359304 | tf_op jit(solution)/shard_map/ppermute | solution.py:302
  116.3 20.0 %collective-permute-start.9 = (bf16[512,768]{1,0:T(8,128)(2,1)}, bf16[512,768]{1,0:T(8,128)(2,1)}, u32[]{:S(2)}, u32[]{:S(2)}) collective-permute-start(bf16[512,768]{1,0:T(8,128)(2,1)} %add_convert_fusion.4), channel_id=1, source_target_pairs={{0,1},{1,0},{2,3},{3,2},{4,5},{5,4},{6,7},{7,6},{8,9},{9,8},{10,11... | collective-permute-start | bytes 2359304 | tf_op jit(solution)/shard_map/ppermute | solution.py:302
  129.6 8.4 %collective-permute-start.12 = (bf16[512,768]{1,0:T(8,128)(2,1)}, bf16[512,768]{1,0:T(8,128)(2,1)}, u32[]{:S(2)}, u32[]{:S(2)}) collective-permute-start(bf16[512,768]{1,0:T(8,128)(2,1)} %collective-permute-done.11), channel_id=1, source_target_pairs={{0,1},{1,0},{2,3},{3,2},{4,5},{5,4},{6,7},{7,6},{8,9},{9,8},{10,11... | collective-permute-start | bytes 2359304 | tf_op jit(solution)/shard_map/ppermute | solution.py:302
  159.0 4.4 %collective-permute-start.19 = (bf16[512,768]{1,0:T(8,128)(2,1)S(1)}, bf16[512,768]{1,0:T(8,128)(2,1)S(1)}, u32[]{:S(2)}, u32[]{:S(2)}) collective-permute-start(bf16[512,768]{1,0:T(8,128)(2,1)S(1)} %convolution_convert_fusion), channel_id=1, source_target_pairs={{0,1},{1,0},{2,3},{3,2},{4,5},{5,4},{6,7},{7,6},{8,9},{9,8},{10,11... | collective-permute-start | bytes 2359304 | tf_op jit(solution)/shard_map/ppermute | solution.py:302
  160.4 5.0 %collective-permute-start.13 = (bf16[512,768]{1,0:T(8,128)(2,1)S(1)}, bf16[512,768]{1,0:T(8,128)(2,1)S(1)}, u32[]{:S(2)}, u32[]{:S(2)}) collective-permute-start(bf16[512,768]{1,0:T(8,128)(2,1)S(1)} %convolution_convert_fusion.2), channel_id=1, source_target_pairs={{0,1},{1,0},{2,3},{3,2},{4,5},{5,4},{6,7},{7,6},{8,9},{9,8},{10,11... | collective-permute-start | bytes 2359304 | tf_op jit(solution)/shard_map/ppermute | solution.py:302
  160.5 8.3 %collective-permute-start.16 = (bf16[512,768]{1,0:T(8,128)(2,1)S(1)}, bf16[512,768]{1,0:T(8,128)(2,1)S(1)}, u32[]{:S(2)}, u32[]{:S(2)}) collective-permute-start(bf16[512,768]{1,0:T(8,128)(2,1)S(1)} %convolution_convert_fusion.1), channel_id=1, source_target_pairs={{0,1},{1,0},{2,3},{3,2},{4,5},{5,4},{6,7},{7,6},{8,9},{9,8},{10,11... | collective-permute-start | bytes 2359304 | tf_op jit(solution)/shard_map/ppermute | solution.py:302
  163.3 22.3 %collective-permute-start.10 = (bf16[512,768]{1,0:T(8,128)(2,1)S(1)}, bf16[512,768]{1,0:T(8,128)(2,1)S(1)}, u32[]{:S(2)}, u32[]{:S(2)}) collective-permute-start(bf16[512,768]{1,0:T(8,128)(2,1)S(1)} %convolution_convert_fusion.3), channel_id=1, source_target_pairs={{0,1},{1,0},{2,3},{3,2},{4,5},{5,4},{6,7},{7,6},{8,9},{9,8},{10,11... | collective-permute-start | bytes 2359304 | tf_op jit(solution)/shard_map/ppermute | solution.py:302
  164.2 20.5 %collective-permute-start.20 = (bf16[512,768]{1,0:T(8,128)(2,1)S(1)}, bf16[512,768]{1,0:T(8,128)(2,1)S(1)}, u32[]{:S(2)}, u32[]{:S(2)}) collective-permute-start(bf16[512,768]{1,0:T(8,128)(2,1)S(1)} %add_convert_fusion.2), channel_id=1, source_target_pairs={{0,2},{1,3},{2,0},{3,1},{4,6},{5,7},{6,4},{7,5},{8,10},{9,11},{10,... | collective-permute-start | bytes 2359304 | tf_op jit(solution)/shard_map/ppermute | solution.py:307
  166.2 34.8 %collective-permute-start.14 = (bf16[512,768]{1,0:T(8,128)(2,1)S(1)}, bf16[512,768]{1,0:T(8,128)(2,1)S(1)}, u32[]{:S(2)}, u32[]{:S(2)}) collective-permute-start(bf16[512,768]{1,0:T(8,128)(2,1)S(1)} %add_convert_fusion.3), channel_id=1, source_target_pairs={{0,2},{1,3},{2,0},{3,1},{4,6},{5,7},{6,4},{7,5},{8,10},{9,11},{10,... | collective-permute-start | bytes 2359304 | tf_op jit(solution)/shard_map/ppermute | solution.py:307
  168.8 16.7 %copy-start.43 = (f32[512]{0:T(512)S(1)}, f32[512]{0:T(512)}, u32[]{:S(2)}) copy-start(f32[512]{0:T(512)} %copy-done.42) | copy-start | bytes 6148
  168.8 32.2 %copy-start.49 = (f32[768]{0:T(1024)S(1)}, f32[768]{0:T(1024)}, u32[]{:S(2)}) copy-start(f32[768]{0:T(1024)} %param.28) | copy-start | bytes 9220
  204.3 8.9 %collective-permute-start.21 = (bf16[512,768]{1,0:T(8,128)(2,1)S(1)}, bf16[512,768]{1,0:T(8,128)(2,1)S(1)}, u32[]{:S(2)}, u32[]{:S(2)}) collective-permute-start(bf16[512,768]{1,0:T(8,128)(2,1)S(1)} %get-tuple-element.100), channel_id=1, source_target_pairs={{0,1},{1,0},{2,3},{3,2},{4,5},{5,4},{6,7},{7,6},{8,9},{9,8},{10,11... | collective-permute-start | bytes 2359304 | tf_op jit(solution)/shard_map/ppermute | solution.py:302
  218.9 16.8 %copy-start.17 = (bf16[512,768]{1,0:T(8,128)(2,1)S(1)}, bf16[512,768]{1,0:T(8,128)(2,1)}, u32[]{:S(2)}) copy-start(bf16[512,768]{1,0:T(8,128)(2,1)} %copy-done.15) | copy-start | bytes 2359300
  218.9 16.8 %copy-start.21 = (bf16[512,768]{1,0:T(8,128)(2,1)S(1)}, bf16[512,768]{1,0:T(8,128)(2,1)}, u32[]{:S(2)}) copy-start(bf16[512,768]{1,0:T(8,128)(2,1)} %copy-done.19) | copy-start | bytes 2359300
  255.3 2.9 copy-start.54
  255.3 2.9 copy-start.59
  255.3 4.2 %copy-start.36 = (bf16[1024,192]{1,0:T(8,128)(2,1)S(1)}, bf16[1024,192]{1,0:T(8,128)(2,1)}, u32[]{:S(2)}) copy-start(bf16[1024,192]{1,0:T(8,128)(2,1)} %get-tuple-element.42.refs_7_) | copy-start | bytes 1179652
  265.3 54.1 %collective-permute-start.22 = (bf16[768,768]{1,0:T(8,128)(2,1)S(1)}, bf16[768,768]{1,0:T(8,128)(2,1)}, u32[]{:S(2)}, u32[]{:S(2)}) collective-permute-start(bf16[768,768]{1,0:T(8,128)(2,1)S(1)} %pad_maximum_fusion.7), channel_id=1, source_target_pairs={{0,2},{1,3},{2,0},{3,1},{4,6},{5,7},{6,4},{7,5},{8,10},{9,11},{10,... | collective-permute-start | bytes 3538952 | tf_op jit(solution)/shard_map/ppermute | solution.py:307
  268.0 3.3 copy-start.9
  275.8 43.7 %copy-start.29 = (f32[768,192]{1,0:T(8,128)S(1)}, f32[768,192]{1,0:T(8,128)}, u32[]{:S(2)}) copy-start(f32[768,192]{1,0:T(8,128)} %fusion.88) | copy-start | bytes 1769476
  315.1 4.3 %copy-start.30 = (f32[768,192]{1,0:T(8,128)S(1)}, f32[768,192]{1,0:T(8,128)}, u32[]{:S(2)}) copy-start(f32[768,192]{1,0:T(8,128)} %fusion.87) | copy-start | bytes 1769476
  315.1 4.3 %copy-start.31 = (f32[768,192]{1,0:T(8,128)S(1)}, f32[768,192]{1,0:T(8,128)}, u32[]{:S(2)}) copy-start(f32[768,192]{1,0:T(8,128)} %fusion.89) | copy-start | bytes 1769476
  374.9 5.7 %copy-start.13 = (bf16[768,384]{1,0:T(8,128)(2,1)S(1)}, bf16[768,384]{1,0:T(8,128)(2,1)}, u32[]{:S(2)}) copy-start(bf16[768,384]{1,0:T(8,128)(2,1)} %get-tuple-element.50) | copy-start | bytes 1769476
  381.1 7.0 %copy-start.1 = (bf16[768,768]{1,0:T(8,128)(2,1)S(1)}, bf16[768,768]{1,0:T(8,128)(2,1)}, u32[]{:S(2)}) copy-start(bf16[768,768]{1,0:T(8,128)(2,1)} %param.25) | copy-start | bytes 3538948
  382.9 4.3 %copy-start.14 = (bf16[512,768]{1,0:T(8,128)(2,1)S(1)}, bf16[512,768]{1,0:T(8,128)(2,1)}, u32[]{:S(2)}) copy-start(bf16[512,768]{1,0:T(8,128)(2,1)} %get-tuple-element.171) | copy-start | bytes 2359300
  (37 other events, 58.0 us)
Sparse Core Ops, SparseCore 0:
  206.0 109.0 all-reduce.3
where the time goes:
time: 402 us; the launch traced here: 395 us
  Pallas kernels  113 us (28%)
  waiting for transfers between devices  101 us (25%)
  matrix products  60.6 us (15%)
  local copies, waits for them, and re-layouts  44.6 us (11%)
  other arithmetic  35.2 us (9%)
  starting transfers between devices  24 us (6%)
  between operations  16.5 us (4%)
    ppermute x8, waiting for transfers between devices, swap_chip(): return lax.ppermute(x, 'tensor', [(i, i ^ 2) for i in range(n)])  55.6 us
    pallas_call x1, Pallas kernels, finish(): pl.pallas_call(lambda *refs: finish_kernel(n, chunk, piece, *refs), in_sp...  51.6 us
    psum x1, waiting for transfers between devices, shards(): lax.psum(jnp.concatenate([up_grad, down_grad], 0).astype(bf16), 'dp')  39.4 us
    pallas_call x2, Pallas kernels, attend_back(): pl.pallas_call(lambda *refs: bwd_kernel(heads, *refs), grid=(back,), in_s...  33.7 us
    dot_general x18, matrix products, mm(): lax.dot_general(a, b, (((1,), (0,)), ((), ())), preferred_element_type=f32)  27.7 us
    unnamed x132, local copies, waits for them, and re-layouts  18 us
    dot_general x13, matrix products, mm_tn(): lax.dot_general(a, b, (((0,), (0,)), ((), ())), preferred_element_type=f32)  17.7 us
    pallas_call x1, Pallas kernels, attend_first(): pl.pallas_call(lambda *refs: fwd_first_kernel(heads, *refs), grid=(n // B...  15.5 us
  transfers between devices with their start and end apart: 24, of which 7 were waited for; matrix products, arithmetic and copies ran while one was open for 24% of the time, Pallas kernels for 16%

commit v1 on v0

--- a/solution.py
+++ b/solution.py
@@ -287,10 +287,6 @@
     centre = source - jnp.mean(source, -1, keepdims=True)
     spread = jnp.mean(centre * centre, -1, keepdims=True)
     return centre * lax.rsqrt(spread + epsilon) * scales + offset
-
-
-def gelu_tanh(source):
-    return jax.nn.gelu(source, approximate=True)
 
 
 def mm_tn(a, b):
@@ -525,6 +521,215 @@
         name="finish",
     )(gb, ga, small, *grads1, *grads2, dsel, w1, w2, sel_w, hidden, gain, gmid)
 
+def norm_parts(x):
+    centre = x - jnp.mean(x, -1, keepdims=True)
+    r = lax.rsqrt(jnp.mean(centre * centre, -1, keepdims=True) + epsilon)
+    return centre * r, r
+
+
+def norm_back(e, xhat, r):
+    return r * (e - jnp.mean(e, -1, keepdims=True) - xhat * jnp.mean(e * xhat, -1, keepdims=True))
+
+
+def gelu_pair(u):
+    k = math.sqrt(2.0 / math.pi)
+    square = u * u
+    t = jnp.tanh(k * u * (1.0 + 0.044715 * square))
+    act = 0.5 * u * (1.0 + t)
+    slope = 0.5 * (1.0 + t) + 0.5 * u * (1.0 - t * t) * (k * (1.0 + 3.0 * 0.044715 * square))
+    return act, slope
+
+
+def feed_kernel(
+    o1, o2, wo1, wo2, hidden, g0, g1, g2, g3, vecs, up, down,
+    rows_out, gmid, partial, branch_x, grads, sums,
+    inner, gs, act, gpre, mid, attn_send, attn_recv,
+    near_send, near_recv, far_send, far_recv, x_send, x_recv,
+    bn_send, bn_recv, bf_send, bf_recv, gin,
+    g_sem, a_s, a_r, i_s, i_r, x_s, x_r, f_s, f_r, n_s, n_r, c_s, c_r, r_s, r_r, b_s, b_r, o_s, o_r,
+):
+    me = lax.axis_index("tensor")
+    odd = lax.rem(me, 2)
+    core = me + 1 - 2 * odd
+    far = lax.rem(me + 2, 4)
+    rows = hidden.shape[0]
+    pieces = rows // BLK
+    loads = [pltpu.make_async_copy(g, gs.at[i], g_sem.at[i]) for i, g in enumerate((g0, g1, g2, g3))]
+    for c in loads:
+        c.start()
+    meet([{"tensor": core}, {"tensor": far}])
+    out_bias, gain, shift, down_bias, up_bias = (vecs[j : j + 1, :] for j in range(5))
+
+    def attn(start):
+        part = pl.ds(pl.multiple_of(start, BLK), BLK)
+        return mm(o1[part, :], wo1[...]) + mm(o2[part, :], wo2[...])
+
+    sends = []
+    attn_copies = []
+    for c in range(pieces):
+        here = pl.ds(c * BLK, BLK)
+        attn_send[here, :] = attn((1 - odd) * rows + c * BLK).astype(bf16)
+        attn_copies.append(send(attn_send.at[here], attn_recv.at[here], a_s.at[c], a_r.at[c], tensor=core))
+    inner_copies, far_copies = [], []
+    for c in range(pieces):
+        here = pl.ds(c * BLK, BLK)
+        mine = attn(odd * rows + c * BLK)
+        attn_copies[c].wait_recv()
+        m = hidden[here, :].astype(f32) + (mine + attn_recv[here, :].astype(f32)) + out_bias
+        mid[here, :] = m
+        xhat, r = norm_parts(m)
+        inner[0, here, :] = (xhat * gain + shift).astype(bf16)
+        far_copies.append(send(inner.at[0, here], inner.at[2, here], x_s.at[c], x_r.at[c], tensor=far))
+        inner_copies.append(send(inner.at[0, here], inner.at[1, here], i_s.at[c], i_r.at[c], tensor=core))
+    sends += attn_copies + inner_copies + far_copies
+    for c in loads:
+        c.wait()
+    sums[...] = jnp.zeros_like(sums)
+
+    def feed(slot, start):
+        part = pl.ds(pl.multiple_of(start, BLK), BLK)
+        pre = mm(inner[slot, part, :], up[...]) + up_bias
+        a, slope = gelu_pair(pre)
+        act[slot, part, :] = a.astype(bf16)
+        gp = (mm_nt(gs[slot, part, :], down[...]) * slope).astype(bf16)
+        gpre[slot, part, :] = gp
+        sums[4:5, :] += jnp.sum(gp.astype(f32), 0, keepdims=True)
+
+    def near(c, _):
+        feed(0, c * BLK)
+        return 0
+
+    lax.fori_loop(0, pieces, near, 0)
+    for c in range(pieces):
+        inner_copies[c].wait_recv()
+
+    def near_other(c, _):
+        part = pl.ds(pl.multiple_of(c * BLK, BLK), BLK)
+        feed(1, c * BLK)
+        near_send[part, :] = mm_nt(gpre[1, part, :], up[...]).astype(bf16)
+        bn_send[part, :] = mm(act[1, part, :], down[...]).astype(bf16)
+        return 0
+
+    lax.fori_loop(0, pieces, near_other, 0)
+    near_copy = send(near_send, near_recv, n_s.at[0], n_r.at[0], tensor=core)
+    branch_copy = send(bn_send, bn_recv, n_s.at[1], n_r.at[1], tensor=core)
+
+    def near_own(c, _):
+        part = pl.ds(pl.multiple_of(c * BLK, BLK), BLK)
+        gin[part, :] = mm_nt(gpre[0, part, :], up[...])
+        partial[part, :] = mid[part, :] + mm(act[0, part, :], down[...]) + down_bias
+        return 0
+
+    lax.fori_loop(0, pieces, near_own, 0)
+
+    passed, crossed, back = [], [], []
+    for c in range(pieces):
+        here = pl.ds(c * BLK, BLK)
+        far_copies[c].wait_recv()
+        passed.append(send(inner.at[2, here], inner.at[3, here], f_s.at[c], f_r.at[c], tensor=core))
+        feed(2, c * BLK)
+        passed[c].wait_recv()
+        feed(3, c * BLK)
+        far_send[here, :] = mm_nt(gpre[3, here, :], up[...]).astype(bf16)
+        crossed.append(send(far_send.at[here], far_recv.at[here], c_s.at[c], c_r.at[c], tensor=core))
+        g = mm_nt(gpre[2, here, :], up[...])
+        crossed[c].wait_recv()
+        x_send[here, :] = (g + far_recv[here, :].astype(f32)).astype(bf16)
+        back.append(send(x_send.at[here], x_recv.at[here], r_s.at[c], r_r.at[c], tensor=far))
+    for c in range(pieces):
+        here = pl.ds(c * BLK, BLK)
+        bf_send[here, :] = mm(act[3, here, :], down[...]).astype(bf16)
+    far_branch = send(bf_send, bf_recv, b_s, b_r, tensor=core)
+    depth = up.shape[0]
+
+    def weights(j, _):
+        part = pl.ds(pl.multiple_of(j * BLK, BLK), BLK)
+        total = mm_tn(inner[0, :, part], gpre[0])
+        other = mm_tn(act[0, :, part], gs[0])
+        for s in range(1, 4):
+            total = total + mm_tn(inner[s, :, part], gpre[s])
+            other = other + mm_tn(act[s, :, part], gs[s])
+        grads[part, :] = total.astype(bf16)
+        grads[pl.ds(pl.multiple_of(depth + j * BLK, BLK), BLK), :] = other.astype(bf16)
+        return 0
+
+    for j in range(depth // BLK):
+        weights(j, 0)
+    far_branch.wait_recv()
+    for c in range(pieces):
+        here = pl.ds(c * BLK, BLK)
+        b = mm(act[2, here, :], down[...])
+        branch_x[here, :] = (b + bf_recv[here, :].astype(f32)).astype(bf16)
+    near_copy.wait_recv()
+    branch_copy.wait_recv()
+    partial[...] += bn_recv[...].astype(f32)
+    rows_copies = []
+    for c in range(pieces):
+        here = pl.ds(c * BLK, BLK)
+        xhat, r = norm_parts(mid[here, :])
+        back[c].wait_recv()
+        g = gin[here, :] + near_recv[here, :].astype(f32) + x_recv[here, :].astype(f32)
+        g_out = gs[0, here, :].astype(f32)
+        gm = g_out + norm_back(g * gain, xhat, r)
+        gmid[here, :] = gm
+        there = pl.ds(pl.multiple_of(odd * rows + c * BLK, BLK), BLK)
+        ga = gm.astype(bf16)
+        rows_out[there, :] = ga
+        rows_copies.append(
+            send(rows_out.at[there], rows_out.at[there], o_s.at[c], o_r.at[c], tensor=core)
+        )
+        sums[0:1, :] += jnp.sum(g * xhat, 0, keepdims=True)
+        sums[1:2, :] += jnp.sum(g, 0, keepdims=True)
+        sums[2:3, :] += jnp.sum(ga.astype(f32), 0, keepdims=True)
+        sums[3:4, :] += jnp.sum(g_out, 0, keepdims=True)
+    for c in rows_copies:
+        c.wait_recv()
+    for c in sends + passed + crossed + back + rows_copies + [near_copy, branch_copy, far_branch]:
+        c.wait_send()
+
+
+def feed_forward(o1, o2, wo1, wo2, hidden, gs, vecs, up, down):
+    rows, depth = hidden.shape
+    width = up.shape[1]
+    pieces = rows // BLK
+    vmem = pl.BlockSpec(memory_space=pltpu.VMEM)
+    anyw = pl.BlockSpec(memory_space=pl.ANY)
+    dma = pltpu.SemaphoreType.DMA
+    wide = pltpu.VMEM((rows, depth), bf16)
+    each = [dma((pieces,))] * 2
+    return pl.pallas_call(
+        feed_kernel,
+        in_specs=[vmem] * 5 + [anyw] * 4 + [vmem] * 3,
+        out_specs=[vmem] * 6,
+        out_shape=[
+            jax.ShapeDtypeStruct((2 * rows, depth), bf16),
+            jax.ShapeDtypeStruct((rows, depth), f32),
+            jax.ShapeDtypeStruct((rows, depth), f32),
+            jax.ShapeDtypeStruct((rows, depth), bf16),
+            jax.ShapeDtypeStruct((depth + width, depth), bf16),
+            jax.ShapeDtypeStruct((8, depth), f32),
+        ],
+        scratch_shapes=[
+            pltpu.VMEM((4, rows, depth), bf16),
+            pltpu.VMEM((4, rows, depth), bf16),
+            pltpu.VMEM((4, rows, width), bf16),
+            pltpu.VMEM((4, rows, width), bf16),
+            pltpu.VMEM((rows, depth), f32),
+            wide, wide, wide, wide, wide, wide, wide, wide, wide, wide, wide, wide,
+            pltpu.VMEM((rows, depth), f32),
+            dma((4,)),
+            *each, *each, *each, *each,
+            dma((2,)), dma((2,)),
+            *each, *each,
+            dma, dma,
+            *each,
+        ],
+        compiler_params=pltpu.CompilerParams(
+            collective_id=1, has_side_effects=True, vmem_limit_bytes=62 * 1024 * 1024
+        ),
+        name="feed_forward",
+    )(o1, o2, wo1, wo2, hidden, *gs, vecs, up, down)
+
 
 def shards(
     hidden_in,
@@ -555,12 +760,6 @@
         second = jnp.where(odd == 0, other, mine)
         return jnp.concatenate([first, second], 0)
 
-    def my_half(x):
-        return lax.dynamic_slice_in_dim(x, odd * rows, rows, 0)
-
-    def other_half(x):
-        return lax.dynamic_slice_in_dim(x, (1 - odd) * rows, rows, 0)
-
     sel_w = jnp.concatenate([qkv_weight[0][:, :HD], qkv_weight[1][:, :HD]], 1)
     sel_b = qv_bias[:1, :HD]
     sel_w = jnp.where(me == 0, sel_w, lax.ppermute(sel_w, "tensor", [(0, 2)]))
@@ -578,9 +777,9 @@
 
     grad_out = out_grad.astype(f32) * live
     grad_branch = grad_out.astype(bf16)
-    grad_near = join(grad_branch, swap_core(grad_branch))
+    grad_core = swap_core(grad_branch)
     grad_far = swap_chip(grad_branch)
-    grad_far = join(grad_far, swap_core(grad_far))
+    grad_cross = lax.ppermute(grad_branch, "tensor", [(i, i ^ 3) for i in range(ranks)])
 
     def project(weights, bias):
         q = (mm(normed, weights[0]) + bias[0]).astype(bf16)
@@ -595,48 +794,12 @@
     q2, k2, v2 = project(qkv_far, bias_far)
     o2, lse2 = attend_next(q2, k2, v2, fence)
 
-    def attn_out(part):
-        return mm(part(o1), out_weight) + mm(part(o2), out_far)
-
-    attn_given = swap_core(attn_out(other_half).astype(bf16))
-    middle = residual + (attn_out(my_half) + attn_given.astype(f32)) + out_bias
-    inner, ln2_back = jax.vjp(layer_norm, middle, ln2_gain, ln2_shift)
-    inner = inner.astype(bf16)
-    inner_near = join(inner, swap_core(inner))
-    inner_far = swap_chip(inner)
-    inner_far = join(inner_far, swap_core(inner_far))
-
-    def feed(inner_rows, grad_rows):
-        pre = mm(inner_rows, up_weight) + up_bias.astype(f32)
-        act, gelu_back = jax.vjp(gelu_tanh, pre)
-        grad_act = mm_nt(grad_rows, down_weight)
-        grad_pre = gelu_back(grad_act)[0].astype(bf16)
-        return act.astype(bf16), grad_pre
-
-    act_near, pre_near = feed(inner_near, grad_near)
-    act_far, pre_far = feed(inner_far, grad_far)
-
-    def gather_sum(near, far, weight, product):
-        far_given = swap_core(product(other_half(far), weight).astype(bf16))
-        far_sum = product(my_half(far), weight) + far_given.astype(f32)
-        from_chip = swap_chip(far_sum.astype(bf16))
-        near_given = swap_core(product(other_half(near), weight).astype(bf16))
-        return product(my_half(near), weight) + near_given.astype(f32) + from_chip.astype(f32)
-
-    grad_inner = gather_sum(pre_near, pre_far, up_weight, mm_nt)
-    branch = gather_sum(act_near, act_far, down_weight, mm)
-    output = (live * (middle + branch + down_bias)).astype(bf16)
-
-    down_grad = mm_tn(act_near, grad_near) + mm_tn(act_far, grad_far)
-    up_grad = mm_tn(inner_near, pre_near) + mm_tn(inner_far, pre_far)
-    up_bias_grad = jnp.sum(pre_near, 0, dtype=f32) + jnp.sum(pre_far, 0, dtype=f32)
-
-    grad_norm2, ln2_gain_grad, ln2_shift_grad = ln2_back(grad_inner)
-    grad_middle = grad_out + grad_norm2
-    grad_attn = grad_middle.astype(bf16)
-    out_bias_grad = jnp.sum(grad_attn, 0, dtype=f32)
-    down_bias_grad = jnp.sum(grad_out, 0)
-    attn_rows = join(grad_attn, swap_core(grad_attn))
+    vecs = jnp.stack([out_bias, ln2_gain, ln2_shift, down_bias, up_bias.astype(f32)])
+    attn_rows, grad_middle, partial, branch_x, ffn_part, sums = feed_forward(
+        o1, o2, out_weight, out_far, hidden_in,
+        (grad_branch, grad_core, grad_far, grad_cross), vecs, up_weight, down_weight,
+    )
+    output = (live * (partial + swap_chip(branch_x).astype(f32))).astype(bf16)
 
     go2 = mm_nt(attn_rows, out_far).astype(bf16)
     go1 = mm_nt(attn_rows, out_weight).astype(bf16)
@@ -660,7 +823,7 @@
     block_b = jnp.pad(jnp.concatenate([block[:, : 2 * width], sel_grad], 1), fill).astype(bf16)
     block_a = jnp.pad(block[:, 2 * width :], fill).astype(bf16)
 
-    ffn_grad = lax.psum(jnp.concatenate([up_grad, down_grad], 0).astype(bf16), "dp").astype(f32)
+    ffn_grad = lax.psum(ffn_part, "dp").astype(f32)
 
     def bias_of(dq, dv):
         return jnp.stack([jnp.sum(dq, 0, dtype=f32), jnp.sum(dv, 0, dtype=f32)])
@@ -672,16 +835,16 @@
         + jnp.where(slot == me ^ 2, bias_of(dq2, dv2)[None], 0.0)
         + jnp.where(slot == 0, sel_bias[None], 0.0)
     )
-    up_parts = jnp.where(slot[:, 0] == me, up_bias_grad[None], 0.0)
-    none = jnp.zeros_like(out_bias_grad)
+    up_parts = jnp.where(slot[:, 0] == me, sums[4:5], 0.0)
+    none = jnp.zeros((depth,), f32)
     small = jnp.concatenate(
         [
             none,
             none,
-            out_bias_grad,
-            ln2_gain_grad,
-            ln2_shift_grad,
-            down_bias_grad,
+            sums[2],
+            sums[0],
+            sums[1],
+            sums[3],
             up_parts.reshape(-1),
             qv_parts.reshape(-1),
         ]

time: 402 us -> 336 us (0.84)
  the two profiles are of different devices: /device:TPU:0 before, /device:TPU:30 now
where the time goes in v1:
time: 336 us; the launch traced here: 330 us
  Pallas kernels  182 us (54%)
  waiting for transfers between devices  38.4 us (11%)
  matrix products  35.3 us (11%)
  local copies, waits for them, and re-layouts  26.2 us (8%)
  other arithmetic  18.2 us (5%)
  between operations  16.5 us (5%)
  starting transfers between devices  13.1 us (4%)
    pallas_call x1, Pallas kernels, finish(): pl.pallas_call(lambda *refs: finish_kernel(n, chunk, piece, *refs), in_sp...  74.1 us
    pallas_call x1, Pallas kernels, feed_forward(): pl.pallas_call(feed_kernel, in_specs=[vmem] * 5 + [anyw] * 4 + [vmem] * 3...  46.6 us
    pallas_call x2, Pallas kernels, attend_back(): pl.pallas_call(lambda *refs: bwd_kernel(heads, *refs), grid=(back,), in_s...  33.7 us
    ppermute x6, waiting for transfers between devices, swap_chip(): return lax.ppermute(x, 'tensor', [(i, i ^ 2) for i in range(n)])  25.2 us
    dot_general x9, matrix products, mm_tn(): lax.dot_general(a, b, (((0,), (0,)), ((), ())), preferred_element_type=f32)  16 us
    pallas_call x1, Pallas kernels, attend_first(): pl.pallas_call(lambda *refs: fwd_first_kernel(heads, *refs), grid=(n // B...  15.3 us
    dot_general x8, matrix products, mm(): lax.dot_general(a, b, (((1,), (0,)), ((), ())), preferred_element_type=f32)  15.1 us
    pallas_call x1, Pallas kernels, attend_next(): pl.pallas_call(lambda *refs: fwd_next_kernel(heads, *refs), grid=(n // BL...  12.6 us
  transfers between devices with their start and end apart: 14, of which 5 were waited for; matrix products, arithmetic and copies ran while one was open for 17% of the time, Pallas kernels for 31%

profile of v1, /device:TPU:30, one launch (start us, length us, event | category | flops | bytes accessed | tf_op | source)
XLA Modules:
  0.0 330.1 jit_solution(8365662854519769637)
XLA Ops:
  7.3 1.4 convert_reduce_fusion
  8.6 1.5 fusion.3
  10.2 1.2 fusion.6
  12.0 1.3 collective-permute-start.3
  13.2 2.7 collective-permute-start.5
  15.9 1.5 copy.79.refs_10_
  18.5 1.4 collective-permute-start.1
  21.6 1.3 constant_dynamic-update-slice_fusion.6
  24.8 1.3 multiply_convert_fusion.1.g0
  26.2 1.3 collective-permute-start.4
  28.7 12.0 %collective-permute-done.1 = bf16[768,128]{1,0:T(8,128)(2,1)} collective-permute-done((bf16[768,128]{1,0:T(8,128)(2,1)}, bf16[768,128]{1,0:T(8,128)(2,1)}, u32[]{:S(2)}, u32[]{:S(2)}) %collective-permute-start.1) | collective-permute-done | bytes 196640 | tf_op jit(solution)/shard_map/ppermute | solution.py:765
  41.8 1.3 collective-permute-start.2
  46.3 1.7 broadcast_select_fusion.1
  48.0 2.6 fusion.8.refs_3_.refs_2_
  50.6 1.4 convolution_convert_fusion.8.refs_5_.refs_7_
  52.0 1.3 fusion.11.refs_4_.refs_6_
  53.2 1.4 convolution_convert_fusion.1.refs_2_.refs_1_
  54.6 1.4 fusion.7.refs_1_.refs_0_
  56.0 15.3 %attend_first.1 = (bf16[1024,192]{1,0:T(8,128)(2,1)}, f32[1024,128]{1,0:T(8,128)}, f32[1024,1024]{1,0:T(8,128)}) custom-call(s32[1]{0:T(128)} %bitcast.2.refs_0_, bf16[1024,192]{1,0:T(8,128)(2,1)} %fusion.7.refs_1_.refs_0_, bf16[1024,192]{1,0:T(8,128)(2,1)} %convolution_convert_fusion.1.refs_2_.refs_1_, bf16[1024,192]{1,0:T(8,128)(2,1)} %fusion.8.refs_3_.refs_2_, ...), custom_call_target="tpu_custom_call" | custom-call | flops 1610612736 | bytes 8388608 | tf_op jit(solution)/shard_map/attend_first/pallas_call | solution.py:124
  71.4 2.4 fusion.9.refs_0_
  73.7 2.4 fusion.10.refs_2_
  76.1 2.4 convolution_convert_fusion.refs_1_
  78.4 12.6 %attend_next.1 = (bf16[1024,192]{1,0:T(8,128)(2,1)}, f32[1024,128]{1,0:T(8,128)}) custom-call(bf16[1024,192]{1,0:T(8,128)(2,1)} %fusion.9.refs_0_, bf16[1024,192]{1,0:T(8,128)(2,1)} %convolution_convert_fusion.refs_1_, bf16[1024,192]{1,0:T(8,128)(2,1)} %fusion.10.refs_2_, f32[1024,1024]{1,0:T(8,128)} %get-tuple-element.40.refs_3_.refs_5_), custom_call_target="tpu_custom_call" | custom-call | flops 1610612736 | bytes 8388608 | tf_op jit(solution)/shard_map/attend_next/pallas_call | solution.py:150
  91.1 46.6 %feed_forward.1 = (bf16[1024,768]{1,0:T(8,128)(2,1)}, f32[512,768]{1,0:T(8,128)}, f32[512,768]{1,0:T(8,128)}, bf16[512,768]{1,0:T(8,128)(2,1)}, bf16[1536,768]{1,0:T(8,128)(2,1)}, /*index=5*/f32[8,768]{1,0:T(8,128)}) custom-call(bf16[1024,192]{1,0:T(8,128)(2,1)} %get-tuple-element.39.o1, bf16[1024,192]{1,0:T(8,128)(2,1)} %get-tuple-element.41.o2, ...), custom_call_target="tpu_custom_call" | custom-call | tf_op jit(solution)/shard_map/feed_forward/pallas_call | solution.py:700
  137.8 2.6 convolution_convert_fusion.3
  140.9 1.6 convolution_convert_fusion.2
  143.6 16.8 %attend_back.3 = (bf16[1024,192]{1,0:T(8,128)(2,1)}, bf16[1024,192]{1,0:T(8,128)(2,1)}, bf16[1024,192]{1,0:T(8,128)(2,1)}, f32[1024,64]{1,0:T(8,128)}, f32[1024,64]{1,0:T(8,128)}) custom-call(bf16[1024,192]{1,0:T(8,128)(2,1)} %fusion.9.refs_0_, bf16[1024,192]{1,0:T(8,128)(2,1)} %convolution_convert_fusion.refs_1_, bf16[1024,192]{1,0:T(8,128)(2,1)} %fusion.10.refs_2_, ...), custom_call_target="tpu_custom_call" | custom-call | flops 4831838208 | bytes 8388608 | tf_op jit(solution)/shard_map/attend_back/pallas_call | solution.py:241
  160.4 2.3 convolution_convert_fusion.5
  162.8 1.2 convolution_convert_fusion.7
  165.2 16.8 %attend_back.2 = (bf16[1024,192]{1,0:T(8,128)(2,1)}, bf16[1024,192]{1,0:T(8,128)(2,1)}, bf16[1024,192]{1,0:T(8,128)(2,1)}, f32[1024,64]{1,0:T(8,128)}, f32[1024,64]{1,0:T(8,128)}) custom-call(bf16[1024,192]{1,0:T(8,128)(2,1)} %fusion.7.refs_1_.refs_0_, bf16[1024,192]{1,0:T(8,128)(2,1)} %convolution_convert_fusion.1.refs_2_.refs_1_, ...), custom_call_target="tpu_custom_call" | custom-call | flops 4831838208 | bytes 8388608 | tf_op jit(solution)/shard_map/attend_back/pallas_call | solution.py:241
  182.0 2.6 fusion.18
  184.6 1.5 fusion.20
  186.9 1.1 collective-permute-start.11
  189.0 1.3 convolution_convert_fusion.9
  190.4 1.1 copy.97
  191.6 1.2 convolution_convert_fusion.6
  192.8 1.1 copy.96
  196.2 2.8 fusion.19
  199.6 2.5 copy.101.refs_11_
  202.2 2.5 fusion.26
  204.7 3.0 collective-permute-done.11
  207.7 2.4 multiply_convert_fusion
  210.1 22.2 %collective-permute-done.12 = bf16[768,768]{1,0:T(8,128)(2,1)S(1)} collective-permute-done((bf16[768,768]{1,0:T(8,128)(2,1)S(1)}, bf16[768,768]{1,0:T(8,128)(2,1)S(1)}, u32[]{:S(2)}, u32[]{:S(2)}) %collective-permute-start.12) | collective-permute-done | bytes 1179680 | tf_op jit(solution)/shard_map/ppermute | solution.py:303
  234.8 74.1 %finish.1 = (bf16[768,384]{1,0:T(8,128)(2,1)}, bf16[768,384]{1,0:T(8,128)(2,1)}, f32[128,128]{1,0:T(8,128)}, bf16[512,768]{1,0:T(8,128)(2,1)}) custom-call(bf16[768,512]{1,0:T(8,128)(2,1)} %pad_maximum_fusion.2.refs_0_, bf16[768,384]{1,0:T(8,128)(2,1)} %get-tuple-element.117.refs_1_, f32[128,128]{1,0:T(8,128)} %pad.9.refs_2_, ...), custom_call_target="tpu_custom_call" | custom-call | tf_op jit(solution)/shard_map/finish/pallas_call | solution.py:484
  310.5 1.3 convert_bitcast_fusion
  312.3 1.8 copy.102
  316.5 1.4 slice_bitcast_fusion.11
  317.9 4.2 %fusion.21 = (f32[768,768]{1,0:T(8,128)}, f32[768,768]{1,0:T(8,128)}) fusion(bf16[1536,768]{1,0:T(8,128)(2,1)} %all-reduce.4.cloned.1.call-done), kind=kLoop, calls=%fused_computation.99 | loop fusion | bytes 9437184 | tf_op jit(solution)/shard_map/slice | solution.py:883
  (182 shorter events, 24.3 us)
Async XLA Ops:
  7.2 3.0 copy-start
  7.2 3.0 copy-start.34
  7.2 3.0 copy-start.32
  7.2 4.2 %copy-start.42 = (f32[2,192]{1,0:T(2,128)S(1)}, f32[2,192]{1,0:T(2,128)}, u32[]{:S(2)}) copy-start(f32[2,192]{1,0:T(2,128)} %param.20) | copy-start | bytes 4612
  7.2 310.6 %all-reduce.4.cloned.1.call-start = ((), (), s32[]{:S(2)}) async-start(), calls=%async_computation | async-start | bytes 4718592 | tf_op jit(solution)/shard_map/psum | solution.py:826
  11.4 33.8 %collective-permute-start = (bf16[512,768]{1,0:T(8,128)(2,1)}, bf16[512,768]{1,0:T(8,128)(2,1)}, u32[]{:S(2)}, u32[]{:S(2)}) collective-permute-start(bf16[512,768]{1,0:T(8,128)(2,1)} %fusion.6), channel_id=1, source_target_pairs={{0,1},{1,0},{2,3},{3,2},{4,5},{5,4},{6,7},{7,6},{8,9},{9,8},{10,11... | collective-permute-start | bytes 2359304 | tf_op jit(solution)/shard_map/ppermute | solution.py:298
  11.4 30.4 %collective-permute-start.6 = (f32[2,192]{1,0:T(2,128)S(1)}, f32[2,192]{1,0:T(2,128)S(1)}, u32[]{:S(2)}, u32[]{:S(2)}) collective-permute-start(f32[2,192]{1,0:T(2,128)S(1)} %copy-done.42), channel_id=1, source_target_pairs={{0,2},{1,3},{2,0},{3,1},{4,6},{5,7},{6,4},{7,5},{8,10},{9,11},{10,... | collective-permute-start | bytes 4616 | tf_op jit(solution)/shard_map/ppermute | solution.py:303
  12.0 14.2 %collective-permute-start.3 = (f32[1,64]{1,0:T(1,128)S(1)}, f32[1,64]{1,0:T(1,128)S(1)}, u32[]{:S(2)}, u32[]{:S(2)}) collective-permute-start(f32[1,64]{1,0:T(1,128)S(1)} %slice.151), channel_id=1, source_target_pairs={{0,2},{4,6},{8,10},{12,14},{16,18},{20,22},{24,26},{28,30}} | collective-permute-start | bytes 776 | tf_op jit(solution)/shard_map/ppermute | solution.py:766
  13.2 58.1 %collective-permute-start.5 = (bf16[3,768,192]{1,2,0:T(8,128)(2,1)}, bf16[3,768,192]{1,2,0:T(8,128)(2,1)}, u32[]{:S(2)}, u32[]{:S(2)}) collective-permute-start(bf16[3,768,192]{1,2,0:T(8,128)(2,1)} %param.19), channel_id=1, source_target_pairs={{0,2},{1,3},{2,0},{3,1},{4,6},{5,7},{6,4},{7,5},{8,10},{9,11},{10,... | collective-permute-start | bytes 2654216 | tf_op jit(solution)/shard_map/ppermute | solution.py:303
  17.5 37.1 %copy-start.1 = (bf16[3,768,192]{2,1,0:T(8,128)(2,1)}, bf16[3,768,192]{2,1,0:T(8,128)(2,1)S(1)}, u32[]{:S(2)}) copy-start(bf16[3,768,192]{2,1,0:T(8,128)(2,1)S(1)} %copy.79.refs_10_) | copy-start | bytes 2654212
  17.5 3.5 %copy-start.45 = (s32[2]{0:T(128)S(1)}, s32[2]{0:T(128)}, u32[]{:S(2)}) copy-start(s32[2]{0:T(128)} %param.16) | copy-start | bytes 28
  17.5 4.1 %copy-start.36 = (f32[768]{0:T(1024)S(1)}, f32[768]{0:T(1024)}, u32[]{:S(2)}) copy-start(f32[768]{0:T(1024)} %param.22) | copy-start | bytes 9220
  17.6 8.5 %copy-start.37 = (f32[768]{0:T(1024)S(1)}, f32[768]{0:T(1024)}, u32[]{:S(2)}) copy-start(f32[768]{0:T(1024)} %param.23) | copy-start | bytes 9220
  17.6 8.5 %copy-start.38 = (f32[768]{0:T(1024)S(1)}, f32[768]{0:T(1024)}, u32[]{:S(2)}) copy-start(f32[768]{0:T(1024)} %param.24) | copy-start | bytes 9220
  17.6 8.6 %copy-start.39 = (f32[768]{0:T(1024)S(1)}, f32[768]{0:T(1024)}, u32[]{:S(2)}) copy-start(f32[768]{0:T(1024)} %param.28) | copy-start | bytes 9220
  17.6 9.9 %copy-start.44 = (bf16[768]{0:T(1024)(128)(2,1)S(1)}, bf16[768]{0:T(1024)(128)(2,1)}, u32[]{:S(2)}) copy-start(bf16[768]{0:T(1024)(128)(2,1)} %param.26) | copy-start | bytes 4612
  18.5 26.8 %copy-start.28 = (bf16[192,768]{1,0:T(8,128)(2,1)S(1)}, bf16[192,768]{1,0:T(8,128)(2,1)}, u32[]{:S(2)}) copy-start(bf16[192,768]{1,0:T(8,128)(2,1)} %wo1.1) | copy-start | bytes 884740
  18.5 22.2 %collective-permute-start.1 = (bf16[768,128]{1,0:T(8,128)(2,1)}, bf16[768,128]{1,0:T(8,128)(2,1)}, u32[]{:S(2)}, u32[]{:S(2)}) collective-permute-start(bf16[768,128]{1,0:T(8,128)(2,1)} %pad_maximum_fusion.4), channel_id=1, source_target_pairs={{0,2},{4,6},{8,10},{12,14},{16,18},{20,22},{24,26},{28,30}} | collective-permute-start | bytes 589832 | tf_op jit(solution)/shard_map/ppermute | solution.py:765
  26.1 21.8 %copy-start.2 = (bf16[512,768]{1,0:T(8,128)(2,1)}, bf16[512,768]{1,0:T(8,128)(2,1)S(1)}, u32[]{:S(2)}) copy-start(bf16[512,768]{1,0:T(8,128)(2,1)S(1)} %multiply_convert_fusion.1.g0) | copy-start | bytes 2359300
  26.2 2.1 collective-permute-start.4
  28.3 62.8 %collective-permute-start.8 = (bf16[512,768]{1,0:T(8,128)(2,1)S(1)}, bf16[512,768]{1,0:T(8,128)(2,1)}, u32[]{:S(2)}, u32[]{:S(2)}) collective-permute-start(bf16[512,768]{1,0:T(8,128)(2,1)S(1)} %multiply_convert_fusion.1.g0), channel_id=1, source_target_pairs={{0,1},{1,0},{2,3},{3,2},{4,5},{5,4},{6,7},{7,6},{8,9},{9,8},{10,11... | collective-permute-start | bytes 2359304 | tf_op jit(solution)/shard_map/ppermute | solution.py:298
  40.7 50.4 %collective-permute-start.9 = (bf16[512,768]{1,0:T(8,128)(2,1)S(1)}, bf16[512,768]{1,0:T(8,128)(2,1)}, u32[]{:S(2)}, u32[]{:S(2)}) collective-permute-start(bf16[512,768]{1,0:T(8,128)(2,1)S(1)} %multiply_convert_fusion.1.g0), channel_id=1, source_target_pairs={{0,2},{1,3},{2,0},{3,1},{4,6},{5,7},{6,4},{7,5},{8,10},{9,11},{10,... | collective-permute-start | bytes 2359304 | tf_op jit(solution)/shard_map/ppermute | solution.py:303
  41.8 2.4 collective-permute-start.2
  44.1 47.0 %collective-permute-start.10 = (bf16[512,768]{1,0:T(8,128)(2,1)S(1)}, bf16[512,768]{1,0:T(8,128)(2,1)}, u32[]{:S(2)}, u32[]{:S(2)}) collective-permute-start(bf16[512,768]{1,0:T(8,128)(2,1)S(1)} %multiply_convert_fusion.1.g0), channel_id=1, source_target_pairs={{0,3},{1,2},{2,1},{3,0},{4,7},{5,6},{6,5},{7,4},{8,11},{9,10},{10,... | collective-permute-start | bytes 2359304 | tf_op jit(solution)/shard_map/ppermute | solution.py:782
  45.2 6.7 %copy-start.20 = (bf16[768,128]{1,0:T(8,128)(2,1)}, bf16[768,128]{1,0:T(8,128)(2,1)S(1)}, u32[]{:S(2)}) copy-start(bf16[768,128]{1,0:T(8,128)(2,1)S(1)} %broadcast_select_fusion.3.refs_12_) | copy-start | bytes 589828
  45.3 45.8 %collective-permute-start.7 = (bf16[192,768]{1,0:T(8,128)(2,1)S(1)}, bf16[192,768]{1,0:T(8,128)(2,1)}, u32[]{:S(2)}, u32[]{:S(2)}) collective-permute-start(bf16[192,768]{1,0:T(8,128)(2,1)S(1)} %copy-done.28), channel_id=1, source_target_pairs={{0,2},{1,3},{2,0},{3,1},{4,6},{5,7},{6,4},{7,5},{8,10},{9,11},{10,... | collective-permute-start | bytes 884744 | tf_op jit(solution)/shard_map/ppermute | solution.py:303
  47.9 6.7 %copy-start.11 = (bf16[512,768]{1,0:T(8,128)(2,1)}, bf16[512,768]{1,0:T(8,128)(2,1)S(1)}, u32[]{:S(2)}) copy-start(bf16[512,768]{1,0:T(8,128)(2,1)S(1)} %get-tuple-element.115) | copy-start | bytes 2359300
  48.0 6.7 %copy-start.14 = (bf16[512,768]{1,0:T(8,128)(2,1)}, bf16[512,768]{1,0:T(8,128)(2,1)S(1)}, u32[]{:S(2)}) copy-start(bf16[512,768]{1,0:T(8,128)(2,1)S(1)} %get-tuple-element.116) | copy-start | bytes 2359300
  56.0 15.3 %copy-start.12 = (bf16[512,768]{1,0:T(8,128)(2,1)S(1)}, bf16[512,768]{1,0:T(8,128)(2,1)}, u32[]{:S(2)}) copy-start(bf16[512,768]{1,0:T(8,128)(2,1)} %copy-done.11) | copy-start | bytes 2359300
  56.0 15.3 %copy-start.15 = (bf16[512,768]{1,0:T(8,128)(2,1)S(1)}, bf16[512,768]{1,0:T(8,128)(2,1)}, u32[]{:S(2)}) copy-start(bf16[512,768]{1,0:T(8,128)(2,1)} %copy-done.14) | copy-start | bytes 2359300
  91.1 46.7 %copy-start.29 = (bf16[192,768]{1,0:T(8,128)(2,1)S(1)}, bf16[192,768]{1,0:T(8,128)(2,1)}, u32[]{:S(2)}) copy-start(bf16[192,768]{1,0:T(8,128)(2,1)} %wo1.1) | copy-start | bytes 884740
  137.7 2.6 copy-start.24
  137.7 2.6 copy-start.48
  143.5 16.9 %copy-start.13 = (bf16[512,768]{1,0:T(8,128)(2,1)S(1)}, bf16[512,768]{1,0:T(8,128)(2,1)}, u32[]{:S(2)}) copy-start(bf16[512,768]{1,0:T(8,128)(2,1)} %copy-done.11) | copy-start | bytes 2359300
  143.5 16.9 %copy-start.16 = (bf16[512,768]{1,0:T(8,128)(2,1)S(1)}, bf16[512,768]{1,0:T(8,128)(2,1)}, u32[]{:S(2)}) copy-start(bf16[512,768]{1,0:T(8,128)(2,1)} %copy-done.14) | copy-start | bytes 2359300
  182.0 2.6 copy-start.5
  184.6 3.4 %copy-start.26 = (f32[1024,64]{1,0:T(8,128)S(1)}, f32[1024,64]{1,0:T(8,128)}, u32[]{:S(2)}) copy-start(f32[1024,64]{1,0:T(8,128)} %get-tuple-element.56) | copy-start | bytes 786436
  184.6 3.4 %copy-start.27 = (f32[1024,64]{1,0:T(8,128)S(1)}, f32[1024,64]{1,0:T(8,128)}, u32[]{:S(2)}) copy-start(f32[1024,64]{1,0:T(8,128)} %get-tuple-element.55) | copy-start | bytes 786436
  186.9 20.7 %collective-permute-start.11 = (bf16[512,768]{1,0:T(8,128)(2,1)}, bf16[512,768]{1,0:T(8,128)(2,1)}, u32[]{:S(2)}, u32[]{:S(2)}) collective-permute-start(bf16[512,768]{1,0:T(8,128)(2,1)} %get-tuple-element.43), channel_id=1, source_target_pairs={{0,2},{1,3},{2,0},{3,1},{4,6},{5,7},{6,4},{7,5},{8,10},{9,11},{10,... | collective-permute-start | bytes 2359304 | tf_op jit(solution)/shard_map/ppermute | solution.py:303
  188.9 2.6 copy-start.22
  194.7 37.6 %collective-permute-start.12 = (bf16[768,768]{1,0:T(8,128)(2,1)S(1)}, bf16[768,768]{1,0:T(8,128)(2,1)S(1)}, u32[]{:S(2)}, u32[]{:S(2)}) collective-permute-start(bf16[768,768]{1,0:T(8,128)(2,1)S(1)} %pad_maximum_fusion.1), channel_id=1, source_target_pairs={{0,2},{1,3},{2,0},{3,1},{4,6},{5,7},{6,4},{7,5},{8,10},{9,11},{10,... | collective-permute-start | bytes 3538952 | tf_op jit(solution)/shard_map/ppermute | solution.py:303
  199.0 3.2 copy-start.21
  202.2 5.5 %copy-start.7 = (f32[512,768]{1,0:T(8,128)S(1)}, f32[512,768]{1,0:T(8,128)}, u32[]{:S(2)}) copy-start(f32[512,768]{1,0:T(8,128)} %get-tuple-element.42) | copy-start | bytes 4718596
  207.7 24.6 %copy-start.17 = (f32[768,192]{1,0:T(8,128)S(1)}, f32[768,192]{1,0:T(8,128)}, u32[]{:S(2)}) copy-start(f32[768,192]{1,0:T(8,128)} %fusion.18) | copy-start | bytes 1769476
  207.7 24.6 %copy-start.18 = (f32[768,192]{1,0:T(8,128)S(1)}, f32[768,192]{1,0:T(8,128)}, u32[]{:S(2)}) copy-start(f32[768,192]{1,0:T(8,128)} %fusion.20) | copy-start | bytes 1769476
  207.7 24.6 %copy-start.19 = (f32[768,192]{1,0:T(8,128)S(1)}, f32[768,192]{1,0:T(8,128)}, u32[]{:S(2)}) copy-start(f32[768,192]{1,0:T(8,128)} %fusion.19) | copy-start | bytes 1769476
  308.9 2.8 copy-start.9
  317.8 4.3 %copy-start.10 = (bf16[512,768]{1,0:T(8,128)(2,1)S(1)}, bf16[512,768]{1,0:T(8,128)(2,1)}, u32[]{:S(2)}) copy-start(bf16[512,768]{1,0:T(8,128)(2,1)} %get-tuple-element.158) | copy-start | bytes 2359300
  (15 other events, 25.1 us)
Sparse Core Ops, SparseCore 0:
  196.2 115.9 all-reduce.3

commit v2 on v1

--- a/solution.py
+++ b/solution.py
@@ -207,79 +207,6 @@
     dskt[:, :cols] += mm(sqt, gsel)
 
 
-def bwd_kernel(heads, q_ref, k_ref, v_ref, do_ref, lse_ref, f_ref, sq_ref, sk_ref,
-               dq_ref, dk_ref, dv_ref, dsq_ref, dsk_ref,
-               dq_scr, dkt, dvt, dskt, later, fsum, qt, dot_):
-    g = pl.program_id(0)
-    n = k_ref.shape[0] // BLK
-
-    @pl.when(g == 0)
-    def _():
-        dkt[...] = jnp.zeros_like(dkt)
-        dvt[...] = jnp.zeros_like(dvt)
-        dskt[...] = jnp.zeros_like(dskt)
-        later[...] = jnp.zeros_like(later)
-
-    for i in range(n):
-
-        @pl.when(g == n - 1 - i)
-        def _():
-            bwd_block(i, heads, q_ref, k_ref, v_ref, do_ref, lse_ref, f_ref, sq_ref, sk_ref,
-                      dq_ref, dsq_ref, dq_scr, dkt, dvt, dskt, later, fsum, qt, dot_)
-
-    @pl.when(g == n - 1)
-    def _():
-        dk_ref[...] = dkt[...].T.astype(bf16)
-        dv_ref[...] = dvt[...].T.astype(bf16)
-        dsk_ref[...] = dskt[...].T
-
-
-def attend_back(q, k, v, do, lse, fence, sq, sk):
-    n, width = q.shape
-    heads = width // HD
-    back = n // BLK
-    return pl.pallas_call(
-        lambda *refs: bwd_kernel(heads, *refs),
-        grid=(back,),
-        in_specs=[
-            row_spec(width, back),
-            full_spec(n, width),
-            full_spec(n, width),
-            row_spec(width, back),
-            row_spec(128, back),
-            row_spec(n, back),
-            row_spec(HD, back),
-            full_spec(n, HD),
-        ],
-        out_specs=[
-            row_spec(width, back),
-            full_spec(n, width),
-            full_spec(n, width),
-            row_spec(HD, back),
-            full_spec(n, HD),
-        ],
-        out_shape=[
-            jax.ShapeDtypeStruct((n, width), bf16),
-            jax.ShapeDtypeStruct((n, width), bf16),
-            jax.ShapeDtypeStruct((n, width), bf16),
-            jax.ShapeDtypeStruct((n, HD), f32),
-            jax.ShapeDtypeStruct((n, HD), f32),
-        ],
-        scratch_shapes=[
-            pltpu.VMEM((BLK, width), f32),
-            pltpu.VMEM((width, n), f32),
-            pltpu.VMEM((width, n), f32),
-            pltpu.VMEM((HD, n), f32),
-            pltpu.VMEM((8, n), f32),
-            pltpu.VMEM((BLK, n), f32),
-            pltpu.VMEM((width, BLK), bf16),
-            pltpu.VMEM((width, BLK), bf16),
-        ],
-        name="attend_back",
-        cost_estimate=pl.CostEstimate(flops=18 * n * n * 256, bytes_accessed=8 * n * n, transcendentals=0),
-    )(q, k, v, do, lse, fence, sq, sk)
-
-
 epsilon = 1e-05
 
 
@@ -321,205 +248,6 @@
         pl.semaphore_signal(barrier, inc=1, device_id=where, device_id_type=pl.DeviceIdType.MESH)
     pl.semaphore_wait(barrier, len(devices))
 
-
-def finish_kernel(
-    n, chunk, piece,
-    gb, ga, small_in, dq1, dk1, dv1, dq2, dk2, dv2, dsel, w1, w2, sel_w, hidden, gain, gmid,
-    fb, fa, small_out, input_grad,
-    ng_send, ng_recv, yb, ya, sb, sa, zb, za, own_b, tb,
-    small, ys, ss, zs, ts, out_s,
-    core_s, core_r, y_s, y_r, z_s, z_r, t_s, t_r, az_s, az_r, ay_s, ay_r,
-):
-    idx = lax.axis_index("dp")
-    me = lax.axis_index("tensor")
-    odd = lax.rem(me, 2)
-    par = lax.rem(idx, 2)
-    z = lax.div(idx, 2)
-    m = n // 2
-    half = m * chunk
-    shalf = m * piece
-    rows = hidden.shape[0]
-    ranks = 4
-    core = me + 1 - 2 * odd
-    ydev = idx + 1 - 2 * par
-    peers = [lax.rem(me + d, ranks) for d in range(1, ranks)]
-    zdev = [lax.rem(z + d, m) for d in range(1, m)]
-    meet(
-        [{"tensor": p} for p in peers]
-        + [{"dp": ydev}]
-        + [{"dp": 2 * p + par} for p in zdev]
-    )
-    give = pl.multiple_of((1 - par) * half, half)
-    keep = pl.multiple_of(par * half, half)
-    cyb = send(gb.at[pl.ds(give, half)], yb, y_s.at[0], y_r.at[0], dp=ydev)
-    cya = send(ga.at[pl.ds(give, half)], ya, y_s.at[1], y_r.at[1], dp=ydev)
-
-    def normed_grad(start):
-        part = pl.ds(pl.multiple_of(start, rows), rows)
-        total = mm_nt(dsel[part, :], sel_w[...])
-        for grads, weights in (((dq1, dk1, dv1), w1), ((dq2, dk2, dv2), w2)):
-            for j in range(3):
-                total = total + mm_nt(grads[j][part, :], weights[j])
-        return total
-
-    ng_send[...] = normed_grad((1 - odd) * rows).astype(bf16)
-    ccore = send(ng_send, ng_recv, core_s, core_r, tensor=core)
-    grad = normed_grad(odd * rows)
-    x = hidden[...].astype(f32)
-    centre = x - jnp.mean(x, -1, keepdims=True)
-    r = lax.rsqrt(jnp.mean(centre * centre, -1, keepdims=True) + epsilon)
-    xhat = centre * r
-    ccore.wait_recv()
-    grad = grad + ng_recv[...].astype(f32)
-    e = grad * gain[...]
-    back = r * (e - jnp.mean(e, -1, keepdims=True) - xhat * jnp.mean(e * xhat, -1, keepdims=True))
-    input_grad[...] = (gmid[...] + back).astype(bf16)
-    small[...] = small_in[...]
-    dgain = jnp.sum(grad * xhat, 0, keepdims=True)
-    dshift = jnp.sum(grad, 0, keepdims=True)
-    lines = dgain.shape[1] // 128
-    for j in range(lines):
-        small[j : j + 1, :] = dgain[:, j * 128 : (j + 1) * 128]
-        small[lines + j : lines + j + 1, :] = dshift[:, j * 128 : (j + 1) * 128]
-    sgive = pl.multiple_of((1 - par) * shalf, shalf)
-    skeep = pl.multiple_of(par * shalf, shalf)
-    cys = send(small.at[pl.ds(sgive, shalf)], ys, y_s.at[2], y_r.at[2], dp=ydev)
-
-    def z_stage(total, recv, size, k):
-        return [
-            send(
-                total.at[pl.ds(pl.multiple_of(zdev[d] * size, size), size)],
-                recv.at[d],
-                z_s.at[k, d],
-                z_r.at[k, d],
-                dp=2 * zdev[d] + par,
-            )
-            for d in range(m - 1)
-        ]
-
-    cyb.wait_recv()
-    sb[...] = (gb[pl.ds(keep, half), :].astype(f32) + yb[...].astype(f32)).astype(bf16)
-    czb = z_stage(sb, zb, chunk, 0)
-    cys.wait_recv()
-    ss[...] = small[pl.ds(skeep, shalf), :] + ys[...]
-    czs = z_stage(ss, zs, piece, 2)
-    cya.wait_recv()
-    sa[...] = (ga[pl.ds(keep, half), :].astype(f32) + ya[...].astype(f32)).astype(bf16)
-    cza = z_stage(sa, za, chunk, 1)
-
-    def z_sum(total, recv, size, copies):
-        acc = total[pl.ds(pl.multiple_of(z * size, size), size), :].astype(f32)
-        for d in range(m - 1):
-            copies[d].wait_recv()
-            acc = acc + recv[d].astype(f32)
-        return acc
-
-    acc_b = z_sum(sb, zb, chunk, czb)
-    own_b[...] = acc_b[:, :384]
-    tb[me] = acc_b[:, 384:].astype(bf16)
-    ts[me] = z_sum(ss, zs, piece, czs)
-    ct = []
-    for d in range(ranks - 1):
-        ct.append(send(tb.at[me], tb.at[me], t_s.at[0, d], t_r.at[0, d], tensor=peers[d]))
-        ct.append(send(ts.at[me], ts.at[me], t_s.at[1, d], t_r.at[1, d], tensor=peers[d]))
-    at = par * m + z
-    mine = pl.ds(pl.multiple_of(at * chunk, chunk), chunk)
-    smine = pl.ds(pl.multiple_of(at * piece, piece), piece)
-
-    def spread(full, where, k):
-        out = [
-            send(full.at[where], full.at[where], az_s.at[k, d], az_r.at[k, d], dp=2 * zdev[d] + par)
-            for d in range(m - 1)
-        ]
-        return out, [send(full.at[where], full.at[where], ay_s.at[k, 0], ay_r.at[k, 0], dp=ydev)]
-
-    def forward(full, size, k, copies, ahead):
-        for d in range(m - 1):
-            copies[d].wait_recv()
-            came = par * m + lax.rem(z - (d + 1) + m, m)
-            where = pl.ds(pl.multiple_of(came * size, size), size)
-            ahead.append(
-                send(full.at[where], full.at[where], ay_s.at[k, d + 1], ay_r.at[k, d + 1], dp=ydev)
-            )
-
-    fa[mine, :] = z_sum(sa, za, chunk, cza).astype(bf16)
-    aza, aya = spread(fa, mine, 1)
-    for c in ct:
-        c.wait_recv()
-    sel = tb[0].astype(f32)
-    vec = ts[0]
-    for d in range(1, ranks):
-        sel = sel + tb[d].astype(f32)
-        vec = vec + ts[d]
-    first = jnp.where(me == 0, 1.0, 0.0)
-    lane = lax.broadcasted_iota(jnp.int32, sel.shape, 1)
-    lower = jnp.where(lane < HD, sel, 0.0) * first
-    upper = jnp.where(lane < HD, 0.0, sel) * first
-    fb[mine, :128] = (own_b[:, :128] + lower).astype(bf16)
-    fb[mine, 128:256] = (own_b[:, 128:256] + upper).astype(bf16)
-    fb[mine, 256:] = own_b[:, 256:].astype(bf16)
-    azb, ayb = spread(fb, mine, 0)
-    out_s[smine, :] = vec
-    azs, ays = spread(out_s, smine, 2)
-    forward(fa, chunk, 1, aza, aya)
-    forward(fb, chunk, 0, azb, ayb)
-    forward(out_s, piece, 2, azs, ays)
-    for c in aya + ayb + ays:
-        c.wait_recv()
-    small_out[...] = out_s[...]
-    for c in [cyb, cya, cys, ccore] + czb + cza + czs + ct + aza + azb + azs + aya + ayb + ays:
-        c.wait_send()
-
-
-def finish(n, gb, ga, small, grads1, grads2, dsel, w1, w2, sel_w, hidden, gain, gmid):
-    m = n // 2
-    chunk = gb.shape[0] // n
-    piece = small.shape[0] // n
-    rows, depth = hidden.shape
-    half, shalf = m * chunk, m * piece
-    wb, wa = gb.shape[1], ga.shape[1]
-    ranks = 4
-    vmem = pl.BlockSpec(memory_space=pltpu.VMEM)
-    dma = pltpu.SemaphoreType.DMA
-    return pl.pallas_call(
-        lambda *refs: finish_kernel(n, chunk, piece, *refs),
-        in_specs=[vmem] * 16,
-        out_specs=[vmem] * 4,
-        out_shape=[
-            jax.ShapeDtypeStruct((n * chunk, wb - 128), bf16),
-            jax.ShapeDtypeStruct((n * chunk, wa), bf16),
-            jax.ShapeDtypeStruct(small.shape, f32),
-            jax.ShapeDtypeStruct((rows, depth), bf16),
-        ],
-        scratch_shapes=[
-            pltpu.VMEM((rows, depth), bf16),
-            pltpu.VMEM((rows, depth), bf16),
-            pltpu.VMEM((half, wb), bf16),
-            pltpu.VMEM((half, wa), bf16),
-            pltpu.VMEM((half, wb), bf16),
-            pltpu.VMEM((half, wa), bf16),
-            pltpu.VMEM((m - 1, chunk, wb), bf16),
-            pltpu.VMEM((m - 1, chunk, wa), bf16),
-            pltpu.VMEM((chunk, wb - 128), f32),
-            pltpu.VMEM((ranks, chunk, 128), bf16),
-            pltpu.VMEM(small.shape, f32),
-            pltpu.VMEM((shalf, 128), f32),
-            pltpu.VMEM((shalf, 128), f32),
-            pltpu.VMEM((m - 1, piece, 128), f32),
-            pltpu.VMEM((ranks, piece, 128), f32),
-            pltpu.VMEM(small.shape, f32),
-            dma, dma,
-            dma((3,)), dma((3,)),
-            dma((3, m - 1)), dma((3, m - 1)),
-            dma((2, 3)), dma((2, 3)),
-            dma((3, m - 1)), dma((3, m - 1)),
-            dma((3, m)), dma((3, m)),
-        ],
-        compiler_params=pltpu.CompilerParams(
-            collective_id=0, has_side_effects=True, vmem_limit_bytes=60 * 1024 * 1024
-        ),
-        name="finish",
-    )(gb, ga, small, *grads1, *grads2, dsel, w1, w2, sel_w, hidden, gain, gmid)
 
 def norm_parts(x):
     centre = x - jnp.mean(x, -1, keepdims=True)
@@ -730,6 +458,319 @@
         name="feed_forward",
     )(o1, o2, wo1, wo2, hidden, *gs, vecs, up, down)
 
+def back_kernel(
+    n, chunk, piece, depth,
+    q1, k1, v1, lse1, q2, k2, v2, lse2, fence, sq, sk, rows_in, o1, o2, wo1, wo2,
+    normed, w1, w2, sel_w, hidden, gain, gmid, small_in, up_g, down_g,
+    fu, fd, fb, fa, small_out, input_grad,
+    go, dq1, dk1, dv1, dq2, dk2, dv2, dsq1, dsk1, dsq2, dsk2,
+    dq_scr, dkt, dvt, dskt, later, fsum, qt, dot_,
+    dsel, ng_send, ng_recv, far_s, far_r, faro_s, faro_r, gb, ga,
+    yu, yd, yb, ya, ys, su, sd, sb, sa, ss, zu, zd, zb, za, zs,
+    own_b, tb, ts, small, out_s,
+    core_s, core_r, f_s, f_r, y_s, y_r, z_s, z_r, t_s, t_r, az_s, az_r, ay_s, ay_r,
+):
+    idx = lax.axis_index("dp")
+    me = lax.axis_index("tensor")
+    odd = lax.rem(me, 2)
+    par = lax.rem(idx, 2)
+    z = lax.div(idx, 2)
+    m = n // 2
+    rows = hidden.shape[0]
+    seq_len = k1.shape[0]
+    width = q1.shape[1]
+    heads = width // HD
+    ranks = 4
+    core = me + 1 - 2 * odd
+    far = lax.rem(me + 2, ranks)
+    ydev = idx + 1 - 2 * par
+    peers = [lax.rem(me + d, ranks) for d in range(1, ranks)]
+    zdev = [lax.rem(z + d, m) for d in range(1, m)]
+    meet(
+        [{"tensor": p} for p in peers]
+        + [{"dp": ydev}]
+        + [{"dp": 2 * p + par} for p in zdev]
+    )
+    at = par * m + z
+    source = (gb, ga, small, up_g, down_g)
+    yrecv = (yb, ya, ys, yu, yd)
+    ysum = (sb, sa, ss, su, sd)
+    zrecv = (zb, za, zs, zu, zd)
+    full = (fb, fa, out_s, fu, fd)
+    size = (chunk, chunk, piece, chunk, chunk)
+    done = []
+
+    def block(start, k):
+        return pl.ds(pl.multiple_of(start * size[k], size[k]), size[k])
+
+    def y_start(k):
+        half = m * size[k]
+        give = pl.ds(pl.multiple_of((1 - par) * half, half), half)
+        copy = send(source[k].at[give], yrecv[k], y_s.at[k], y_r.at[k], dp=ydev)
+        done.append(copy)
+        return copy
+
+    def y_finish(k, copy):
+        half = m * size[k]
+        keep = pl.ds(pl.multiple_of(par * half, half), half)
+        copy.wait_recv()
+        total = source[k][keep, :].astype(f32) + yrecv[k][...].astype(f32)
+        ysum[k][...] = total.astype(ysum[k].dtype)
+        copies = [
+            send(
+                ysum[k].at[block(zdev[d], k)], zrecv[k].at[d], z_s.at[k, d], z_r.at[k, d],
+                dp=2 * zdev[d] + par,
+            )
+            for d in range(m - 1)
+        ]
+        done.extend(copies)
+        return copies
+
+    def z_finish(k, copies):
+        acc = ysum[k][block(z, k), :].astype(f32)
+        for d in range(m - 1):
+            copies[d].wait_recv()
+            acc = acc + zrecv[k][d].astype(f32)
+        return acc
+
+    def spread(k):
+        mine = full[k].at[block(at, k)]
+        out = [
+            send(mine, mine, az_s.at[k, d], az_r.at[k, d], dp=2 * zdev[d] + par)
+            for d in range(m - 1)
+        ]
+        own = send(mine, mine, ay_s.at[k, 0], ay_r.at[k, 0], dp=ydev)
+        done.extend(out + [own])
+        return out, [own]
+
+    def forward(k, out, ahead):
+        for d in range(m - 1):
+            out[d].wait_recv()
+            came = full[k].at[block(par * m + lax.rem(z - (d + 1) + m, m), k)]
+            copy = send(came, came, ay_s.at[k, d + 1], ay_r.at[k, d + 1], dp=ydev)
+            ahead.append(copy)
+            done.append(copy)
+
+    cu = y_start(3)
+    faro_s[...] = mm_tn(o2[...], rows_in[...]).astype(bf16)
+    cfo = send(faro_s, faro_r, f_s.at[0], f_r.at[0], tensor=far)
+
+    def attention(q, k, v, lse, wo, dq, dk, dv, dsq, dsk, hooks):
+        for j in range(seq_len // BLK):
+            here = pl.ds(j * BLK, BLK)
+            go[here, :] = mm_nt(rows_in[here, :], wo[...]).astype(bf16)
+        for r in (dkt, dvt, dskt, later):
+            r[...] = jnp.zeros_like(r)
+        for i in reversed(range(seq_len // BLK)):
+            here = pl.ds(i * BLK, BLK)
+            bwd_block(
+                i, heads, q.at[here], k, v, go.at[here], lse.at[here], fence.at[here],
+                sq.at[here], sk, dq.at[here], dsq.at[here],
+                dq_scr, dkt, dvt, dskt, later, fsum, qt, dot_,
+            )
+            if i in hooks:
+                hooks[i]()
+        dk[...] = dkt[...].T.astype(bf16)
+        dv[...] = dvt[...].T.astype(bf16)
+        dsk[...] = dskt[...].T
+
+    last = seq_len // BLK - 1
+    keep = {}
+
+    def start_down():
+        keep["yd"] = y_start(4)
+
+    attention(q2, k2, v2, lse2, wo2, dq2, dk2, dv2, dsq2, dsk2, {last: start_down})
+    for j, d in enumerate((dq2, dk2, dv2)):
+        far_s[:, j * width : (j + 1) * width] = mm_tn(normed[...], d[...]).astype(bf16)
+    cfar = send(far_s, far_r, f_s.at[1], f_r.at[1], tensor=far)
+    keep["zu"] = y_finish(3, cu)
+
+    def down_z():
+        keep["zd"] = y_finish(4, keep["yd"])
+
+    def up_spread():
+        fu[block(at, 3), :] = z_finish(3, keep["zu"]).astype(bf16)
+        keep["au"] = spread(3)
+
+    attention(q1, k1, v1, lse1, wo1, dq1, dk1, dv1, dsq1, dsk1, {last: down_z, last - 1: up_spread})
+    dsel[:, :HD] = (dsq1[...] + dsq2[...]).astype(bf16)
+    dsel[:, HD:] = (dsk1[...] + dsk2[...]).astype(bf16)
+
+    def normed_grad(start):
+        part = pl.ds(pl.multiple_of(start, rows), rows)
+        total = mm_nt(dsel[part, :], sel_w[...])
+        for grads, weights in (((dq1, dk1, dv1), w1), ((dq2, dk2, dv2), w2)):
+            for j in range(3):
+                total = total + mm_nt(grads[j][part, :], weights[j])
+        return total
+
+    ng_send[...] = normed_grad((1 - odd) * rows).astype(bf16)
+    ccore = send(ng_send, ng_recv, core_s, core_r, tensor=core)
+    gq = mm_tn(normed[...], dq1[...])
+    gk = mm_tn(normed[...], dk1[...])
+    gs = mm_tn(normed[...], dsel[...])
+    cfar.wait_recv()
+    if n * chunk > depth:
+        gb[...] = jnp.zeros_like(gb)
+        ga[...] = jnp.zeros_like(ga)
+    real = pl.ds(0, depth)
+    gb[real, :width] = (gq + far_r[:, :width].astype(f32)).astype(bf16)
+    gb[real, width : 2 * width] = (gk + far_r[:, width : 2 * width].astype(f32)).astype(bf16)
+    gb[real, 2 * width :] = gs.astype(bf16)
+    cb = y_start(0)
+    gv = mm_tn(normed[...], dv1[...])
+    ga[real, :width] = (gv + far_r[:, 2 * width :].astype(f32)).astype(bf16)
+    cfo.wait_recv()
+    wide = mm_tn(o1[...], rows_in[...]) + faro_r[...].astype(f32)
+    ga[real, width:] = wide.T.astype(bf16)
+    ca = y_start(1)
+    fd[block(at, 4), :] = z_finish(4, keep["zd"]).astype(bf16)
+    ad = spread(4)
+    forward(3, *keep["au"])
+
+    grad = normed_grad(odd * rows)
+    xhat, r = norm_parts(hidden[...].astype(f32))
+    ccore.wait_recv()
+    grad = grad + ng_recv[...].astype(f32)
+    input_grad[...] = (gmid[...] + norm_back(grad * gain[...], xhat, r)).astype(bf16)
+    small[...] = small_in[...]
+    dgain = jnp.sum(grad * xhat, 0, keepdims=True)
+    dshift = jnp.sum(grad, 0, keepdims=True)
+    lines = depth // 128
+    for j in range(lines):
+        small[j : j + 1, :] = dgain[:, j * 128 : (j + 1) * 128]
+        small[lines + j : lines + j + 1, :] = dshift[:, j * 128 : (j + 1) * 128]
+    base = small_lines(depth, up_g.shape[1]) - 4 * ranks
+    for owner, q, v in ((me, dq1, dv1), (far, dq2, dv2)):
+        for j, d in enumerate((q, v)):
+            total = jnp.sum(d[...].astype(f32), 0, keepdims=True)
+            line = base + 4 * owner + 2 * j
+            small[pl.ds(line, 1), :] = total[:, :128]
+            small[pl.ds(line + 1, 1), : width - 128] = total[:, 128:]
+    total = jnp.sum(dsel[...].astype(f32), 0, keepdims=True)
+    lane = lax.broadcasted_iota(jnp.int32, total.shape, 1)
+    small[base : base + 1, :] += jnp.where(lane < HD, total, 0.0)
+    cs = y_start(2)
+
+    czb = y_finish(0, cb)
+    czs = y_finish(2, cs)
+    cza = y_finish(1, ca)
+    acc_b = z_finish(0, czb)
+    own_b[...] = acc_b[:, : 2 * width]
+    tb[me] = acc_b[:, 2 * width :].astype(bf16)
+    ts[me] = z_finish(2, czs)
+    ct = []
+    for d in range(ranks - 1):
+        ct.append(send(tb.at[me], tb.at[me], t_s.at[0, d], t_r.at[0, d], tensor=peers[d]))
+        ct.append(send(ts.at[me], ts.at[me], t_s.at[1, d], t_r.at[1, d], tensor=peers[d]))
+    done.extend(ct)
+    fa[block(at, 1), :] = z_finish(1, cza).astype(bf16)
+    aa = spread(1)
+    for c in ct:
+        c.wait_recv()
+    sel = tb[0].astype(f32)
+    vec = ts[0]
+    for d in range(1, ranks):
+        sel = sel + tb[d].astype(f32)
+        vec = vec + ts[d]
+    first = jnp.where(me == 0, 1.0, 0.0)
+    lane = lax.broadcasted_iota(jnp.int32, sel.shape, 1)
+    mine = block(at, 0)
+    fb[mine, :128] = (own_b[:, :128] + jnp.where(lane < HD, sel, 0.0) * first).astype(bf16)
+    fb[mine, 128:256] = (own_b[:, 128:256] + jnp.where(lane < HD, 0.0, sel) * first).astype(bf16)
+    fb[mine, 256:] = own_b[:, 256:].astype(bf16)
+    ab = spread(0)
+    out_s[block(at, 2), :] = vec
+    asm = spread(2)
+    forward(4, *ad)
+    forward(1, *aa)
+    forward(0, *ab)
+    forward(2, *asm)
+    for _, ahead in (keep["au"], ad, aa, ab, asm):
+        for c in ahead:
+            c.wait_recv()
+    small_out[...] = out_s[...]
+    for c in done + [cfo, cfar, ccore]:
+        c.wait_send()
+
+
+def small_lines(depth, hidden):
+    return (6 * depth + 4 * hidden) // 128 + 16
+
+
+def go_back(n, set1, set2, fence, sq, sk, rows_in, o1, o2, wo1, wo2, normed, w1, w2, sel_w,
+            hidden, gain, gmid, small, up_g, down_g):
+    m = n // 2
+    chunk = up_g.shape[0] // n
+    piece = small.shape[0] // n
+    rows, depth = hidden.shape
+    seq_len, width = set1[0].shape
+    half, shalf = m * chunk, m * piece
+    ranks = 4
+    wb, wa, wf = 2 * width + 128, 2 * width, up_g.shape[1]
+    vmem = pl.BlockSpec(memory_space=pltpu.VMEM)
+    dma = pltpu.SemaphoreType.DMA
+    args = (*set1, *set2, fence, sq, sk, rows_in, o1, o2, wo1, wo2, normed, w1, w2, sel_w,
+            hidden, gain, gmid, small, up_g, down_g)
+    heads = pltpu.VMEM((seq_len, width), bf16)
+    part = pltpu.VMEM((seq_len, HD), f32)
+    return pl.pallas_call(
+        lambda *refs: back_kernel(n, chunk, piece, depth, *refs),
+        in_specs=[vmem] * len(args),
+        out_specs=[vmem] * 6,
+        out_shape=[
+            jax.ShapeDtypeStruct((n * chunk, wf), bf16),
+            jax.ShapeDtypeStruct((n * chunk, wf), bf16),
+            jax.ShapeDtypeStruct((n * chunk, 2 * width), bf16),
+            jax.ShapeDtypeStruct((n * chunk, wa), bf16),
+            jax.ShapeDtypeStruct(small.shape, f32),
+            jax.ShapeDtypeStruct((rows, depth), bf16),
+        ],
+        scratch_shapes=[
+            heads, heads, heads, heads, heads, heads, heads, part, part, part, part,
+            pltpu.VMEM((BLK, width), f32),
+            pltpu.VMEM((width, seq_len), f32),
+            pltpu.VMEM((width, seq_len), f32),
+            pltpu.VMEM((HD, seq_len), f32),
+            pltpu.VMEM((8, seq_len), f32),
+            pltpu.VMEM((BLK, seq_len), f32),
+            pltpu.VMEM((width, BLK), bf16),
+            pltpu.VMEM((width, BLK), bf16),
+            pltpu.VMEM((seq_len, 128), bf16),
+            pltpu.VMEM((rows, depth), bf16),
+            pltpu.VMEM((rows, depth), bf16),
+            pltpu.VMEM((depth, 3 * width), bf16),
+            pltpu.VMEM((depth, 3 * width), bf16),
+            pltpu.VMEM((width, depth), bf16),
+            pltpu.VMEM((width, depth), bf16),
+            pltpu.VMEM((n * chunk, wb), bf16),
+            pltpu.VMEM((n * chunk, wa), bf16),
+            *[pltpu.VMEM((half, w), bf16) for w in (wf, wf, wb, wa)],
+            pltpu.VMEM((shalf, 128), f32),
+            *[pltpu.VMEM((half, w), bf16) for w in (wf, wf, wb, wa)],
+            pltpu.VMEM((shalf, 128), f32),
+            *[pltpu.VMEM((m - 1, chunk, w), bf16) for w in (wf, wf, wb, wa)],
+            pltpu.VMEM((m - 1, piece, 128), f32),
+            pltpu.VMEM((chunk, 2 * width), f32),
+            pltpu.VMEM((ranks, chunk, 128), bf16),
+            pltpu.VMEM((ranks, piece, 128), f32),
+            pltpu.VMEM(small.shape, f32),
+            pltpu.VMEM(small.shape, f32),
+            dma, dma,
+            dma((2,)), dma((2,)),
+            dma((5,)), dma((5,)),
+            dma((5, m - 1)), dma((5, m - 1)),
+            dma((2, 3)), dma((2, 3)),
+            dma((5, m - 1)), dma((5, m - 1)),
+            dma((5, m)), dma((5, m)),
+        ],
+        compiler_params=pltpu.CompilerParams(
+            collective_id=0, has_side_effects=True, vmem_limit_bytes=63 * 1024 * 1024
+        ),
+        name="go_back",
+    )(*args)
+
 
 def shards(
     hidden_in,
@@ -801,68 +842,32 @@
     )
     output = (live * (partial + swap_chip(branch_x).astype(f32))).astype(bf16)
 
-    go2 = mm_nt(attn_rows, out_far).astype(bf16)
-    go1 = mm_nt(attn_rows, out_weight).astype(bf16)
-    dq2, dk2, dv2, dsq2, dsk2 = attend_back(q2, k2, v2, go2, lse2, fence, sq, sk)
-    dq1, dk1, dv1, dsq1, dsk1 = attend_back(q1, k1, v1, go1, lse1, fence, sq, sk)
-
-    def grad_block(dq, dk, dv, o):
-        return jnp.concatenate(
-            [mm_tn(normed, dq), mm_tn(normed, dk), mm_tn(normed, dv), mm_tn(attn_rows, o)], 1
-        )
-
     n = lax.axis_size("dp")
     width = q1.shape[1]
     depth = normed.shape[1]
+    hidden = up_bias.shape[0]
     chunk = -(-depth // (16 * n)) * 16
-    far_block = swap_chip(grad_block(dq2, dk2, dv2, o2).astype(bf16))
-    block = grad_block(dq1, dk1, dv1, o1) + far_block.astype(f32)
-    dsel = jnp.concatenate([dsq1 + dsq2, dsk1 + dsk2], 1).astype(bf16)
-    sel_grad = mm_tn(normed, dsel)
     fill = ((0, n * chunk - depth), (0, 0))
-    block_b = jnp.pad(jnp.concatenate([block[:, : 2 * width], sel_grad], 1), fill).astype(bf16)
-    block_a = jnp.pad(block[:, 2 * width :], fill).astype(bf16)
-
-    ffn_grad = lax.psum(ffn_part, "dp").astype(f32)
-
-    def bias_of(dq, dv):
-        return jnp.stack([jnp.sum(dq, 0, dtype=f32), jnp.sum(dv, 0, dtype=f32)])
-
-    slot = jnp.arange(ranks)[:, None, None]
-    sel_bias = jnp.pad(jnp.sum(dsel[:, :HD], 0, dtype=f32)[None], ((0, 1), (0, width - HD)))
-    qv_parts = (
-        jnp.where(slot == me, bias_of(dq1, dv1)[None], 0.0)
-        + jnp.where(slot == me ^ 2, bias_of(dq2, dv2)[None], 0.0)
-        + jnp.where(slot == 0, sel_bias[None], 0.0)
+    up_part = jnp.pad(ffn_part[:depth], fill)
+    down_part = jnp.pad(ffn_part[depth:], fill)
+    slot = jnp.arange(ranks)[:, None]
+    up_rows = jnp.where(slot == me, sums[4:5], 0.0)
+    none = jnp.zeros((depth,), f32)
+    small = jnp.concatenate([none, none, sums[2], sums[0], sums[1], sums[3], up_rows.reshape(-1)])
+    small = small.reshape(-1, 128)
+    piece = -(-small_lines(depth, hidden) // (8 * n)) * 8
+    small = jnp.pad(small, ((0, n * piece - small.shape[0]), (0, 0)))
+    full_u, full_d, full_b, full_a, small, input_grad = go_back(
+        n, (q1, k1, v1, lse1), (q2, k2, v2, lse2), fence, sq, sk, attn_rows, o1, o2,
+        out_weight, out_far, normed, qkv_weight, qkv_far, sel_w, hidden_in, ln1_gain[None],
+        grad_middle, small, up_part, down_part,
     )
-    up_parts = jnp.where(slot[:, 0] == me, sums[4:5], 0.0)
-    none = jnp.zeros((depth,), f32)
-    small = jnp.concatenate(
-        [
-            none,
-            none,
-            sums[2],
-            sums[0],
-            sums[1],
-            sums[3],
-            up_parts.reshape(-1),
-            qv_parts.reshape(-1),
-        ]
-    )
-    lines = small.shape[0] // 128
-    piece = -(-lines // (8 * n)) * 8
-    small = jnp.pad(small.reshape(lines, 128), ((0, n * piece - lines), (0, 0)))
-    full_b, full_a, small, input_grad = finish(
-        n, block_b, block_a, small, (dq1, dk1, dv1), (dq2, dk2, dv2), dsel,
-        qkv_weight, qkv_far, sel_w, hidden_in, ln1_gain[None], grad_middle,
-    )
-    small = small[:lines].reshape(-1)
-    vectors = small[: 6 * depth].reshape(6, depth)
-    hidden = up_bias.shape[0]
-    up_all = small[6 * depth : 6 * depth + ranks * hidden].reshape(ranks, hidden)
-    qv_all = small[6 * depth + ranks * hidden :].reshape(ranks, 2, width)
+    vectors = small[: 6 * depth // 128].reshape(6, depth)
+    lines = (6 * depth + ranks * hidden) // 128
+    up_all = small[6 * depth // 128 : lines].reshape(ranks, hidden)
+    qv_all = small[lines : lines + 4 * ranks].reshape(ranks, 2, 256)
     up_bias_grad = lax.dynamic_index_in_dim(up_all, me, 0, keepdims=False)
-    qv_bias_grad = lax.dynamic_index_in_dim(qv_all, me, 0, keepdims=False)
+    qv_bias_grad = lax.dynamic_index_in_dim(qv_all, me, 0, keepdims=False)[:, :width]
     qkv_grad = jnp.stack(
         [full_b[:depth, :width], full_b[:depth, width:], full_a[:depth, :width]]
     ).astype(f32)
@@ -878,9 +883,9 @@
         vectors[2],
         vectors[3],
         vectors[4],
-        ffn_grad[:depth],
+        full_u[:depth].astype(f32),
         up_bias_grad,
-        ffn_grad[depth:],
+        full_d[:depth].astype(f32),
         vectors[5],
     )
 

time: 336 us -> 284 us (0.85)
  the two profiles are of different devices: /device:TPU:30 before, /device:TPU:0 now
where the time goes in v2:
time: 284 us; the launch traced here: 279 us
  Pallas kernels  196 us (69%)
  starting transfers between devices  18.2 us (6%)
  local copies, waits for them, and re-layouts  17.9 us (6%)
  other arithmetic  16.6 us (6%)
  matrix products  15 us (5%)
  waiting for transfers between devices  12.1 us (4%)
    pallas_call x1, Pallas kernels, go_back(): pl.pallas_call(lambda *refs: back_kernel(n, chunk, piece, depth, *refs),...  122 us
    pallas_call x1, Pallas kernels, feed_forward(): pl.pallas_call(feed_kernel, in_specs=[vmem] * 5 + [anyw] * 4 + [vmem] * 3...  46.5 us
    pallas_call x1, Pallas kernels, attend_first(): pl.pallas_call(lambda *refs: fwd_first_kernel(heads, *refs), grid=(n // B...  15.3 us
    dot_general x8, matrix products, mm(): lax.dot_general(a, b, (((1,), (0,)), ((), ())), preferred_element_type=f32)  15 us
    pallas_call x1, Pallas kernels, attend_next(): pl.pallas_call(lambda *refs: fwd_next_kernel(heads, *refs), grid=(n // BL...  12.6 us
    ppermute x1, waiting for transfers between devices, shards(): sel_w = jnp.where(me == 0, sel_w, lax.ppermute(sel_w, 'tensor', [(0, 2)]))  10.9 us
    ppermute x5, starting transfers between devices, swap_chip(): return lax.ppermute(x, 'tensor', [(i, i ^ 2) for i in range(n)])  7.19 us
    unnamed x59, local copies, waits for them, and re-layouts  6.59 us
  transfers between devices with their start and end apart: 12, of which 3 were waited for; matrix products, arithmetic and copies ran while one was open for 15% of the time, Pallas kernels for 54%

profile of v2, /device:TPU:0, one launch (start us, length us, event | category | flops | bytes accessed | tf_op | source)
XLA Modules:
  0.0 278.7 jit_solution(3870765809968378499)
XLA Ops:
  0.7 1.4 convert_reduce_fusion
  2.1 1.5 fusion.2
  3.6 1.2 fusion.5
  5.3 2.5 collective-permute-start.6
  7.8 1.9 collective-permute-start.3
  9.8 1.5 copy.43.refs_17_
  11.6 0.8 pad_maximum_fusion.1
  12.4 4.7 %collective-permute-start.1 = (bf16[768,128]{1,0:T(8,128)(2,1)}, bf16[768,128]{1,0:T(8,128)(2,1)}, u32[]{:S(2)}, u32[]{:S(2)}) collective-permute-start(bf16[768,128]{1,0:T(8,128)(2,1)} %pad_maximum_fusion.1), channel_id=1, source_target_pairs={{0,2},{4,6},{8,10},{12,14},{16,18},{20,22},{24,26},{28,30}} | collective-permute-start | bytes 589832 | tf_op jit(solution)/shard_map/ppermute | solution.py:806
  17.1 0.6 broadcast_in_dim.35.refs_21_
  17.7 0.6 fusion.20
  19.6 1.3 multiply_convert_fusion.1.g0
  21.1 1.3 collective-permute-start.4
  22.4 0.6 stack.39.vecs
  23.5 10.9 %collective-permute-done.1 = bf16[768,128]{1,0:T(8,128)(2,1)} collective-permute-done((bf16[768,128]{1,0:T(8,128)(2,1)}, bf16[768,128]{1,0:T(8,128)(2,1)}, u32[]{:S(2)}, u32[]{:S(2)}) %collective-permute-start.1) | collective-permute-done | bytes 196640 | tf_op jit(solution)/shard_map/ppermute | solution.py:806
  34.4 2.5 collective-permute-start.9
  37.0 1.3 collective-permute-start.2
  38.4 1.0 collective-permute-done.2
  39.4 0.9 collective-permute-start.10
  40.3 1.2 collective-permute-start.7
  41.5 1.7 broadcast_select_fusion.1
  43.2 2.6 fusion.7.refs_3_.refs_2_
  45.8 1.3 fusion.10.refs_4_.refs_9_
  47.1 1.3 convolution_convert_fusion.2.refs_5_.refs_10_
  48.5 1.4 convolution_convert_fusion.1.refs_2_.refs_1_
  49.9 1.4 fusion.6.refs_1_.refs_0_
  51.2 15.3 %attend_first.1 = (bf16[1024,192]{1,0:T(8,128)(2,1)}, f32[1024,128]{1,0:T(8,128)}, f32[1024,1024]{1,0:T(8,128)}) custom-call(s32[1]{0:T(128)} %bitcast.2.refs_0_, bf16[1024,192]{1,0:T(8,128)(2,1)} %fusion.6.refs_1_.refs_0_, bf16[1024,192]{1,0:T(8,128)(2,1)} %convolution_convert_fusion.1.refs_2_.refs_1_, bf16[1024,192]{1,0:T(8,128)(2,1)} %fusion.7.refs_3_.refs_2_, ...), custom_call_target="tpu_custom_call" | custom-call | flops 1610612736 | bytes 8388608 | tf_op jit(solution)/shard_map/attend_first/pallas_call | solution.py:124
  66.6 1.2 pad_maximum_fusion.refs_16_
  67.8 2.3 fusion.8.refs_0_.refs_4_
  70.2 2.3 fusion.9.refs_2_.refs_6_
  72.5 2.3 convolution_convert_fusion.refs_1_.refs_5_
  74.9 12.6 %attend_next.1 = (bf16[1024,192]{1,0:T(8,128)(2,1)}, f32[1024,128]{1,0:T(8,128)}) custom-call(bf16[1024,192]{1,0:T(8,128)(2,1)} %fusion.8.refs_0_.refs_4_, bf16[1024,192]{1,0:T(8,128)(2,1)} %convolution_convert_fusion.refs_1_.refs_5_, bf16[1024,192]{1,0:T(8,128)(2,1)} %fusion.9.refs_2_.refs_6_, f32[1024,1024]{1,0:T(8,128)} %get-tuple-element.32.refs_3_.refs_8_), custom_call_target="tpu_custom_call" | custom-call | flops 1610612736 | bytes 8388608 | tf_op jit(solution)/shard_map/attend_next/pallas_call | solution.py:150
  87.5 0.7 copy-done.11
  88.2 46.5 %feed_forward.1 = (bf16[1024,768]{1,0:T(8,128)(2,1)}, f32[512,768]{1,0:T(8,128)}, f32[512,768]{1,0:T(8,128)}, bf16[512,768]{1,0:T(8,128)(2,1)}, bf16[1536,768]{1,0:T(8,128)(2,1)}, /*index=5*/f32[8,768]{1,0:T(8,128)}) custom-call(bf16[1024,192]{1,0:T(8,128)(2,1)} %get-tuple-element.31.o1.refs_12_, bf16[1024,192]{1,0:T(8,128)(2,1)} %get-tuple-element.33.o2.refs_13_, ...), custom_call_target="tpu_custom_call" | custom-call | tf_op jit(solution)/shard_map/feed_forward/pallas_call | solution.py:428
  134.7 1.0 collective-permute-start.11
  135.7 1.0 slice_reduce_fusion
  136.8 3.5 %fusion.17 = (bf16[768,768]{1,0:T(8,128)(2,1)}, bf16[768,768]{1,0:T(8,128)(2,1)}) fusion(bf16[1536,768]{1,0:T(8,128)(2,1)} %get-tuple-element.41), kind=kLoop, calls=%fused_computation.71 | loop fusion | bytes 4718592 | tf_op jit(solution)/shard_map/slice | solution.py:852
  140.3 0.6 pad.4.refs_23_
  140.9 2.3 copy.54.refs_18_
  143.2 121.7 %go_back.1 = (bf16[768,768]{1,0:T(8,128)(2,1)}, bf16[768,768]{1,0:T(8,128)(2,1)}, bf16[768,384]{1,0:T(8,128)(2,1)}, bf16[768,384]{1,0:T(8,128)(2,1)}, f32[128,128]{1,0:T(8,128)}, /*index=5*/bf16[512,768]{1,0:T(8,128)(2,1)}) custom-call(bf16[1024,192]{1,0:T(8,128)(2,1)} %fusion.6.refs_1_.refs_0_, bf16[1024,192]{1,0:T(8,128)(2,1)} %convolution_convert_fusion.1.refs_2_.refs_1_, ...), custom_call_target="tpu_custom_call" | custom-call | tf_op jit(solution)/shard_map/go_back/pallas_call | solution.py:718
  264.9 1.4 convert_bitcast_fusion
  266.9 1.8 copy.55
  268.7 1.1 copy.56
  270.2 1.6 convert_element_type.85
  271.8 1.6 convert_element_type.86
  273.4 0.6 dynamic-slice_reduce_fusion
  274.6 0.6 slice_bitcast_fusion.11
  275.2 2.3 multiply_convert_fusion
  277.6 0.9 copy.72
  (97 shorter events, 3.2 us)
Async XLA Ops:
  0.6 2.9 %copy-start = (bf16[512,768]{1,0:T(8,128)(2,1)S(1)}, bf16[512,768]{1,0:T(8,128)(2,1)}, u32[]{:S(2)}) copy-start(bf16[512,768]{1,0:T(8,128)(2,1)} %refs_20_.1) | copy-start | bytes 2359300
  0.7 2.9 %copy-start.17 = (f32[768]{0:T(1024)S(1)}, f32[768]{0:T(1024)}, u32[]{:S(2)}) copy-start(f32[768]{0:T(1024)} %param.18) | copy-start | bytes 9220
  0.7 2.9 %copy-start.15 = (f32[768]{0:T(1024)S(1)}, f32[768]{0:T(1024)}, u32[]{:S(2)}) copy-start(f32[768]{0:T(1024)} %param.17) | copy-start | bytes 9220
  0.7 4.7 %copy-start.22 = (f32[2,192]{1,0:T(2,128)S(1)}, f32[2,192]{1,0:T(2,128)}, u32[]{:S(2)}) copy-start(f32[2,192]{1,0:T(2,128)} %param.20) | copy-start | bytes 4612
  4.8 35.5 %collective-permute-start = (bf16[512,768]{1,0:T(8,128)(2,1)}, bf16[512,768]{1,0:T(8,128)(2,1)}, u32[]{:S(2)}, u32[]{:S(2)}) collective-permute-start(bf16[512,768]{1,0:T(8,128)(2,1)} %fusion.5), channel_id=1, source_target_pairs={{0,1},{1,0},{2,3},{3,2},{4,5},{5,4},{6,7},{7,6},{8,9},{9,8},{10,11... | collective-permute-start | bytes 2359304 | tf_op jit(solution)/shard_map/ppermute | solution.py:225
  5.3 31.7 %collective-permute-start.6 = (f32[2,192]{1,0:T(2,128)S(1)}, f32[2,192]{1,0:T(2,128)S(1)}, u32[]{:S(2)}, u32[]{:S(2)}) collective-permute-start(f32[2,192]{1,0:T(2,128)S(1)} %copy-done.22), channel_id=1, source_target_pairs={{0,2},{1,3},{2,0},{3,1},{4,6},{5,7},{6,4},{7,5},{8,10},{9,11},{10,... | collective-permute-start | bytes 4616 | tf_op jit(solution)/shard_map/ppermute | solution.py:230
  7.8 13.2 %collective-permute-start.3 = (f32[1,64]{1,0:T(1,128)S(1)}, f32[1,64]{1,0:T(1,128)S(1)}, u32[]{:S(2)}, u32[]{:S(2)}) collective-permute-start(f32[1,64]{1,0:T(1,128)S(1)} %slice.136), channel_id=1, source_target_pairs={{0,2},{4,6},{8,10},{12,14},{16,18},{20,22},{24,26},{28,30}} | collective-permute-start | bytes 776 | tf_op jit(solution)/shard_map/ppermute | solution.py:807
  9.7 58.1 %collective-permute-start.5 = (bf16[3,768,192]{1,2,0:T(8,128)(2,1)}, bf16[3,768,192]{1,2,0:T(8,128)(2,1)}, u32[]{:S(2)}, u32[]{:S(2)}) collective-permute-start(bf16[3,768,192]{1,2,0:T(8,128)(2,1)} %param.19), channel_id=1, source_target_pairs={{0,2},{1,3},{2,0},{3,1},{4,6},{5,7},{6,4},{7,5},{8,10},{9,11},{10,... | collective-permute-start | bytes 2654216 | tf_op jit(solution)/shard_map/ppermute | solution.py:230
  11.4 38.5 %copy-start.1 = (bf16[3,768,192]{2,1,0:T(8,128)(2,1)}, bf16[3,768,192]{2,1,0:T(8,128)(2,1)S(1)}, u32[]{:S(2)}) copy-start(bf16[3,768,192]{2,1,0:T(8,128)(2,1)S(1)} %copy.43.refs_17_) | copy-start | bytes 2654212
  11.4 6.3 %copy-start.24 = (s32[2]{0:T(128)S(1)}, s32[2]{0:T(128)}, u32[]{:S(2)}) copy-start(s32[2]{0:T(128)} %param.16) | copy-start | bytes 28
  11.4 6.9 %copy-start.18 = (f32[768]{0:T(1024)S(1)}, f32[768]{0:T(1024)}, u32[]{:S(2)}) copy-start(f32[768]{0:T(1024)} %param.22) | copy-start | bytes 9220
  11.5 9.5 %copy-start.19 = (f32[768]{0:T(1024)S(1)}, f32[768]{0:T(1024)}, u32[]{:S(2)}) copy-start(f32[768]{0:T(1024)} %param.23) | copy-start | bytes 9220
  11.5 9.5 %copy-start.20 = (f32[768]{0:T(1024)S(1)}, f32[768]{0:T(1024)}, u32[]{:S(2)}) copy-start(f32[768]{0:T(1024)} %param.24) | copy-start | bytes 9220
  11.5 9.5 %copy-start.21 = (f32[768]{0:T(1024)S(1)}, f32[768]{0:T(1024)}, u32[]{:S(2)}) copy-start(f32[768]{0:T(1024)} %param.28) | copy-start | bytes 9220
  11.5 10.8 %copy-start.23 = (bf16[768]{0:T(1024)(128)(2,1)S(1)}, bf16[768]{0:T(1024)(128)(2,1)}, u32[]{:S(2)}) copy-start(bf16[768]{0:T(1024)(128)(2,1)} %param.26) | copy-start | bytes 4612
  12.4 28.0 %copy-start.10 = (bf16[192,768]{1,0:T(8,128)(2,1)S(1)}, bf16[192,768]{1,0:T(8,128)(2,1)}, u32[]{:S(2)}) copy-start(bf16[192,768]{1,0:T(8,128)(2,1)} %refs_14_.1) | copy-start | bytes 884740
  12.4 22.0 %collective-permute-start.1 = (bf16[768,128]{1,0:T(8,128)(2,1)}, bf16[768,128]{1,0:T(8,128)(2,1)}, u32[]{:S(2)}, u32[]{:S(2)}) collective-permute-start(bf16[768,128]{1,0:T(8,128)(2,1)} %pad_maximum_fusion.1), channel_id=1, source_target_pairs={{0,2},{4,6},{8,10},{12,14},{16,18},{20,22},{24,26},{28,30}} | collective-permute-start | bytes 589832 | tf_op jit(solution)/shard_map/ppermute | solution.py:806
  21.0 22.2 %copy-start.2 = (bf16[512,768]{1,0:T(8,128)(2,1)}, bf16[512,768]{1,0:T(8,128)(2,1)S(1)}, u32[]{:S(2)}) copy-start(bf16[512,768]{1,0:T(8,128)(2,1)S(1)} %multiply_convert_fusion.1.g0) | copy-start | bytes 2359300
  21.1 2.1 collective-permute-start.4
  23.1 64.3 %collective-permute-start.8 = (bf16[512,768]{1,0:T(8,128)(2,1)S(1)}, bf16[512,768]{1,0:T(8,128)(2,1)}, u32[]{:S(2)}, u32[]{:S(2)}) collective-permute-start(bf16[512,768]{1,0:T(8,128)(2,1)S(1)} %multiply_convert_fusion.1.g0), channel_id=1, source_target_pairs={{0,1},{1,0},{2,3},{3,2},{4,5},{5,4},{6,7},{7,6},{8,9},{9,8},{10,11... | collective-permute-start | bytes 2359304 | tf_op jit(solution)/shard_map/ppermute | solution.py:225
  34.4 53.1 %collective-permute-start.9 = (bf16[512,768]{1,0:T(8,128)(2,1)S(1)}, bf16[512,768]{1,0:T(8,128)(2,1)}, u32[]{:S(2)}, u32[]{:S(2)}) collective-permute-start(bf16[512,768]{1,0:T(8,128)(2,1)S(1)} %multiply_convert_fusion.1.g0), channel_id=1, source_target_pairs={{0,2},{1,3},{2,0},{3,1},{4,6},{5,7},{6,4},{7,5},{8,10},{9,11},{10,... | collective-permute-start | bytes 2359304 | tf_op jit(solution)/shard_map/ppermute | solution.py:230
  37.0 2.4 collective-permute-start.2
  39.4 48.1 %collective-permute-start.10 = (bf16[512,768]{1,0:T(8,128)(2,1)S(1)}, bf16[512,768]{1,0:T(8,128)(2,1)}, u32[]{:S(2)}, u32[]{:S(2)}) collective-permute-start(bf16[512,768]{1,0:T(8,128)(2,1)S(1)} %multiply_convert_fusion.1.g0), channel_id=1, source_target_pairs={{0,3},{1,2},{2,1},{3,0},{4,7},{5,6},{6,5},{7,4},{8,11},{9,10},{10,... | collective-permute-start | bytes 2359304 | tf_op jit(solution)/shard_map/ppermute | solution.py:823
  40.3 6.8 %copy-start.13 = (bf16[768,128]{1,0:T(8,128)(2,1)}, bf16[768,128]{1,0:T(8,128)(2,1)S(1)}, u32[]{:S(2)}) copy-start(bf16[768,128]{1,0:T(8,128)(2,1)S(1)} %broadcast_select_fusion.3.refs_19_) | copy-start | bytes 589828
  40.3 47.1 %collective-permute-start.7 = (bf16[192,768]{1,0:T(8,128)(2,1)S(1)}, bf16[192,768]{1,0:T(8,128)(2,1)S(1)}, u32[]{:S(2)}, u32[]{:S(2)}) collective-permute-start(bf16[192,768]{1,0:T(8,128)(2,1)S(1)} %copy-done.10), channel_id=1, source_target_pairs={{0,2},{1,3},{2,0},{3,1},{4,6},{5,7},{6,4},{7,5},{8,10},{9,11},{10,... | collective-permute-start | bytes 884744 | tf_op jit(solution)/shard_map/ppermute | solution.py:230
  43.2 6.7 %copy-start.3 = (bf16[512,768]{1,0:T(8,128)(2,1)}, bf16[512,768]{1,0:T(8,128)(2,1)S(1)}, u32[]{:S(2)}) copy-start(bf16[512,768]{1,0:T(8,128)(2,1)S(1)} %get-tuple-element.83) | copy-start | bytes 2359300
  43.2 6.6 %copy-start.5 = (bf16[512,768]{1,0:T(8,128)(2,1)}, bf16[512,768]{1,0:T(8,128)(2,1)S(1)}, u32[]{:S(2)}) copy-start(bf16[512,768]{1,0:T(8,128)(2,1)S(1)} %get-tuple-element.84) | copy-start | bytes 2359300
  51.2 15.3 %copy-start.4 = (bf16[512,768]{1,0:T(8,128)(2,1)S(1)}, bf16[512,768]{1,0:T(8,128)(2,1)}, u32[]{:S(2)}) copy-start(bf16[512,768]{1,0:T(8,128)(2,1)} %copy-done.3) | copy-start | bytes 2359300
  51.2 15.3 %copy-start.6 = (bf16[512,768]{1,0:T(8,128)(2,1)S(1)}, bf16[512,768]{1,0:T(8,128)(2,1)}, u32[]{:S(2)}) copy-start(bf16[512,768]{1,0:T(8,128)(2,1)} %copy-done.5) | copy-start | bytes 2359300
  87.5 0.7 copy-start.11
  134.7 140.5 %collective-permute-start.11 = (bf16[512,768]{1,0:T(8,128)(2,1)}, bf16[512,768]{1,0:T(8,128)(2,1)}, u32[]{:S(2)}, u32[]{:S(2)}) collective-permute-start(bf16[512,768]{1,0:T(8,128)(2,1)} %get-tuple-element.35), channel_id=1, source_target_pairs={{0,2},{1,3},{2,0},{3,1},{4,6},{5,7},{6,4},{7,5},{8,10},{9,11},{10,... | collective-permute-start | bytes 2359304 | tf_op jit(solution)/shard_map/ppermute | solution.py:230
  264.9 1.4 copy-start.16
  264.9 1.4 copy-start.12
  268.7 1.5 copy-start.9
  270.2 1.7 copy-start.8
  271.8 3.4 %copy-start.7 = (f32[512,768]{1,0:T(8,128)S(1)}, f32[512,768]{1,0:T(8,128)}, u32[]{:S(2)}) copy-start(f32[512,768]{1,0:T(8,128)} %get-tuple-element.34) | copy-start | bytes 4718596
  275.2 2.3 copy-start.14
